TPU v7x, 32 devices: a whole 2x2x4 slice. The times are simulated.
32 devices in a mesh: groups: 2 (over y), ffn: 4 (over x, core), width: 4 (over z).
Axes of the slice: x: 2, y: 2, z: 4, core: 2. Of those that a mesh axis runs over, the one named last changes fastest.
Arguments:
- hidden: bfloat16 [2048, 8192], P(('groups', 'ffn'), 'width'), parts along dimension 0, may hold values from -8.4 to 8.4
- upstream: bfloat16 [2048, 8192], P(('groups', 'ffn'), 'width'), parts along dimension 0, may hold values from -6 to 6
- query_frozen_weight: bfloat16 [8192, 8192], P('width', 'ffn'), may hold values from -0.0625 to 0.0625
- key_value_frozen_weight: bfloat16 [2, 8192, 1024], P(None, 'width', 'ffn'), may hold values from -0.0625 to 0.0625
- output_frozen_weight: bfloat16 [8192, 8192], P('ffn', 'width'), may hold values from -0.0625 to 0.0625
- adapter_down: bfloat16 [6, 16, 8192], P('groups', None, 'width'), parts along dimension 0, may hold values from -0.0625 to 0.0625
- query_up_map: bfloat16 [32, 8192], P('groups', 'ffn'), parts along dimension 0, may hold values from -0.0625 to 0.0625
- key_value_up_maps: bfloat16 [4, 16, 1024], P('groups', None, 'ffn'), parts along dimension 0, may hold values from -0.0625 to 0.0625
- output_down_map: bfloat16 [32, 8192], P('groups', 'ffn'), parts along dimension 0, may hold values from -0.0625 to 0.0625
- output_up: bfloat16 [32, 8192], P('groups', 'width'), parts along dimension 0, may hold values from -0.0625 to 0.0625
Outputs:
- hidden_gradient: bfloat16 [2048, 8192], P(('groups', 'ffn'), 'width'), parts along dimension 0
- down_map_gradient: float32 [6, 16, 8192], P('groups', None, 'width'), parts along dimension 0
- query_up_map_gradient: float32 [32, 8192], P('groups', 'ffn'), parts along dimension 0
- key_value_up_maps_gradient: float32 [4, 16, 1024], P('groups', None, 'ffn'), parts along dimension 0
- output_down_map_gradient: float32 [32, 8192], P('groups', 'ffn'), parts along dimension 0
- output_up_map_gradient: float32 [32, 8192], P('groups', 'width'), parts along dimension 0
There are 2 independent parts, one for each index of `groups`. A program takes and returns all parts, laid end to end along the dimension named above; an argument that names none is the same for every part. Nothing has to cross between parts.
All inputs are finite; a program needn't handle non-finite values.
Results may differ from a plain program's by a relative error of at most 0.04.
Values may be sent and summed in bfloat16 or wider, within the bound.
A program may use at most 128 MiB of HBM per device.

v0:
```python
import functools
import math

import jax
import jax.numpy as jnp
from jax import lax
from jax.experimental import pallas as pl
from jax.experimental.pallas import tpu as pltpu
from jax.sharding import PartitionSpec as P

KV_HEADS = 8
HEAD_DIM = 128
ADAPTER_RANK = 16
BLOCKS = 4
CHUNK_HEADS = 2
PIECES = 2


adapter_scale = 2.0
rope_base = 500000.0


def from_partner(array, axis, bit):
    return lax.ppermute(array, axis, [(i, i ^ 1 << bit) for i in range(lax.axis_size(axis))])


def rotate(values, positions, first_dim, direction):
    columns = values.shape[1]
    head_dims = (first_dim + jnp.arange(columns, dtype=jnp.int32)) % HEAD_DIM
    pair_dims = head_dims - head_dims % 2
    frequency = jnp.exp(pair_dims.astype(jnp.float32) * (-math.log(rope_base) / HEAD_DIM))
    angles = positions.astype(jnp.float32)[:, None] * frequency[None, :]
    is_even = head_dims % 2 == 0
    following = jnp.roll(values, -1, axis=1)
    preceding = jnp.roll(values, 1, axis=1)
    partner = jnp.where(is_even[None, :], -following, preceding)
    return values * jnp.cos(angles) + direction * partner * jnp.sin(angles)


def contract_last(left_side, right_side):
    return lax.dot_general(
        left_side, right_side, (((1,), (1,)), ((), ())), preferred_element_type=jnp.float32
    )


def contract_leading(left_side, right_side):
    return lax.dot_general(
        left_side, right_side, (((0,), (0,)), ((), ())), preferred_element_type=jnp.float32
    )


def shards(
    hidden,
    upstream,
    query_frozen_weight,
    key_value_frozen_weight,
    output_frozen_weight,
    adapter_down,
    query_up_map,
    key_value_up_maps,
    output_down_map,
    output_up,
):
    ffn_count = lax.axis_size("ffn")
    width_count = lax.axis_size("width")
    ffn_index = lax.axis_index("ffn")
    width_index = lax.axis_index("width")
    hidden_rows_full, upstream_gradient_full = (
        lax.all_gather(hidden, "ffn", axis=0, tiled=True),
        lax.all_gather(upstream, "ffn", axis=0, tiled=True),
    )
    token_count = hidden_rows_full.shape[0]
    query_rows = token_count // width_count
    query_cols = query_frozen_weight.shape[1]
    key_cols = key_value_frozen_weight.shape[2]
    row_start = width_index * query_rows
    positions = jnp.arange(token_count, dtype=jnp.int32)
    row_positions = row_start + jnp.arange(query_rows, dtype=jnp.int32)
    query_offset = ffn_index * query_cols
    key_offset = ffn_index * key_cols
    score_scale = 1.0 / math.sqrt(HEAD_DIM)
    down_flattened = adapter_down.reshape(3 * ADAPTER_RANK, adapter_down.shape[2])
    paired = ffn_count > KV_HEADS
    parity = ffn_index % 2
    rank_terms = contract_last(hidden_rows_full, down_flattened)
    upstream_terms = contract_last(upstream_gradient_full, output_up)
    rank_sum, upstream_sum = lax.psum((rank_terms, upstream_terms), "width")
    reduced_hidden = rank_sum.astype(jnp.bfloat16)
    output_reduced = upstream_sum.astype(jnp.bfloat16)
    low_rows = lax.dynamic_slice_in_dim(reduced_hidden, row_start, query_rows, 0)
    output_token_rows = lax.dynamic_slice_in_dim(output_reduced, row_start, query_rows, 0)
    query_part = jnp.dot(hidden_rows_full, query_frozen_weight, preferred_element_type=jnp.float32)
    query_gradient_summed = lax.psum_scatter(
        query_part.astype(jnp.bfloat16), "width", scatter_dimension=0, tiled=True
    ).astype(jnp.float32)
    query_projected = query_gradient_summed + adapter_scale * jnp.dot(
        low_rows[:, :ADAPTER_RANK], query_up_map, preferred_element_type=jnp.float32
    )
    query_states = rotate(query_projected, row_positions, query_offset, 1.0).astype(jnp.bfloat16)
    key_part = jnp.dot(
        hidden_rows_full, key_value_frozen_weight[0], preferred_element_type=jnp.float32
    )
    value_part = jnp.dot(
        hidden_rows_full, key_value_frozen_weight[1], preferred_element_type=jnp.float32
    )
    key_gradient_summed, value_gradient_summed = (
        lax.psum_scatter(
            key_part.astype(jnp.bfloat16), "width", scatter_dimension=0, tiled=True
        ).astype(jnp.float32),
        lax.psum_scatter(
            value_part.astype(jnp.bfloat16), "width", scatter_dimension=0, tiled=True
        ).astype(jnp.float32),
    )
    key_projected = key_gradient_summed + adapter_scale * jnp.dot(
        low_rows[:, ADAPTER_RANK : 2 * ADAPTER_RANK],
        key_value_up_maps[0],
        preferred_element_type=jnp.float32,
    )
    value_projected = value_gradient_summed + adapter_scale * jnp.dot(
        low_rows[:, 2 * ADAPTER_RANK :], key_value_up_maps[1], preferred_element_type=jnp.float32
    )
    key_block = rotate(key_projected, row_positions, key_offset, 1.0).astype(jnp.bfloat16)
    value_block = value_projected.astype(jnp.bfloat16)
    key_states, value_state_rows = (
        lax.all_gather(key_block, "width", axis=0, tiled=True),
        lax.all_gather(value_block, "width", axis=0, tiled=True),
    )
    if paired:
        other_key, other_value = from_partner((key_states, value_state_rows), "ffn", 0)
        key_states = jnp.where(
            parity == 0,
            jnp.concatenate([key_states, other_key], 1),
            jnp.concatenate([other_key, key_states], 1),
        )
        value_state_rows = jnp.where(
            parity == 0,
            jnp.concatenate([value_state_rows, other_value], 1),
            jnp.concatenate([other_value, value_state_rows], 1),
        )
    local_heads = query_cols // HEAD_DIM
    local_groups = key_states.shape[1] // HEAD_DIM
    group_size = local_heads // local_groups
    query_four = query_states.reshape(query_rows, local_groups, group_size, HEAD_DIM)
    key_three = key_states.reshape(token_count, local_groups, HEAD_DIM)
    value_three = value_state_rows.reshape(token_count, local_groups, HEAD_DIM)
    causal = row_positions[:, None] >= positions[None, :]
    scores = (
        jnp.einsum("qkgd,skd->kgqs", query_four, key_three, preferred_element_type=jnp.float32)
        * score_scale
    )
    scores = jnp.where(causal[None, None, :, :], scores, -jnp.inf)
    shifted = jnp.exp(scores - jnp.max(scores, axis=-1, keepdims=True))
    probs = shifted / jnp.sum(shifted, axis=-1, keepdims=True)
    prob_weights = probs.astype(jnp.bfloat16)
    attention_four = jnp.einsum(
        "kgqs,skd->qkgd", prob_weights, value_three, preferred_element_type=jnp.float32
    ).astype(jnp.bfloat16)
    attention_output = attention_four.reshape(query_rows, query_cols)
    out_part = contract_last(upstream_gradient_full, output_frozen_weight)
    output_gradient_summed = lax.psum_scatter(
        out_part.astype(jnp.bfloat16), "width", scatter_dimension=0, tiled=True
    ).astype(jnp.float32)
    attention_output_gradient = (
        output_gradient_summed
        + adapter_scale
        * jnp.dot(output_token_rows, output_down_map, preferred_element_type=jnp.float32)
    ).astype(jnp.bfloat16)
    grad_four = attention_output_gradient.reshape(query_rows, local_groups, group_size, HEAD_DIM)
    prob_grad = jnp.einsum(
        "qkgd,skd->kgqs", grad_four, value_three, preferred_element_type=jnp.float32
    )
    delta = jnp.einsum(
        "qkgd,qkgd->kgq", grad_four, attention_four, preferred_element_type=jnp.float32
    )
    score_grad = (probs * (prob_grad - delta[:, :, :, None]) * score_scale).astype(jnp.bfloat16)
    query_rot_grad = jnp.einsum(
        "kgqs,skd->qkgd", score_grad, key_three, preferred_element_type=jnp.float32
    ).reshape(query_rows, query_cols)
    key_part_grad = jnp.einsum(
        "kgqs,qkgd->skd", score_grad, query_four, preferred_element_type=jnp.float32
    ).reshape(token_count, local_groups * HEAD_DIM)
    value_part_grad = jnp.einsum(
        "kgqs,qkgd->skd", prob_weights, grad_four, preferred_element_type=jnp.float32
    ).reshape(token_count, local_groups * HEAD_DIM)
    query_block_grad = rotate(query_rot_grad, row_positions, query_offset, -1.0).astype(
        jnp.bfloat16
    )

    def own_half(values):
        return lax.dynamic_slice_in_dim(values, parity * key_cols, key_cols, 1)

    def other_half(values):
        return lax.dynamic_slice_in_dim(values, (1 - parity) * key_cols, key_cols, 1)

    key_total, value_total = lax.psum((key_part_grad, value_part_grad), "width")
    if paired:
        sent_key, sent_value = from_partner(
            (other_half(key_total), other_half(value_total)), "ffn", 0
        )
        key_total = own_half(key_total) + sent_key
        value_total = own_half(value_total) + sent_value
    key_rows_gradient = rotate(key_total, positions, key_offset, -1.0).astype(jnp.bfloat16)
    value_rows_gradient = value_total.astype(jnp.bfloat16)
    query_rows_gradient = lax.all_gather(query_block_grad, "width", axis=0, tiled=True)
    input_part = (
        contract_last(query_rows_gradient, query_frozen_weight)
        + contract_last(key_rows_gradient, key_value_frozen_weight[0])
        + contract_last(value_rows_gradient, key_value_frozen_weight[1])
    )
    rank_grad_terms = jnp.concatenate(
        [
            contract_last(query_rows_gradient, query_up_map),
            contract_last(key_rows_gradient, key_value_up_maps[0]),
            contract_last(value_rows_gradient, key_value_up_maps[1]),
        ],
        axis=1,
    )
    rank_gradient = lax.psum(rank_grad_terms, "ffn").astype(jnp.bfloat16)
    input_sum = lax.psum_scatter(
        input_part.astype(jnp.bfloat16), "ffn", scatter_dimension=0, tiled=True
    ).astype(jnp.float32)
    own_rows = token_count // ffn_count
    rank_gradient_token_rows = lax.dynamic_slice_in_dim(
        rank_gradient, ffn_index * own_rows, own_rows, 0
    )
    hidden_gradient = (
        input_sum
        + adapter_scale
        * jnp.dot(rank_gradient_token_rows, down_flattened, preferred_element_type=jnp.float32)
    ).astype(jnp.bfloat16)
    down_map_gradient = (adapter_scale * contract_leading(rank_gradient, hidden_rows_full)).reshape(
        adapter_down.shape
    )
    query_up_map_gradient = adapter_scale * contract_leading(
        reduced_hidden[:, :ADAPTER_RANK], query_rows_gradient
    )
    key_value_up_maps_gradient = adapter_scale * jnp.stack(
        [
            contract_leading(reduced_hidden[:, ADAPTER_RANK : 2 * ADAPTER_RANK], key_rows_gradient),
            contract_leading(reduced_hidden[:, 2 * ADAPTER_RANK :], value_rows_gradient),
        ]
    )
    outer_terms = contract_last(attention_output, output_down_map)
    outer_rows = lax.psum(outer_terms, "ffn").astype(jnp.bfloat16)
    outer_product_rank = lax.all_gather(outer_rows, "width", axis=0, tiled=True)
    output_down_map_gradient = adapter_scale * lax.psum(
        contract_leading(output_token_rows, attention_output), "width"
    )
    output_up_map_gradient = adapter_scale * contract_leading(
        outer_product_rank, upstream_gradient_full
    )
    return (
        hidden_gradient,
        down_map_gradient,
        query_up_map_gradient,
        key_value_up_maps_gradient,
        output_down_map_gradient,
        output_up_map_gradient,
    )


def causal_heads(scale, own_q, add_q, low, up, own_g, add_g, low_g, up_g, key, value, cosine, sine,
                 attention, query_grad, key_grad, value_grad):
    rows, columns = own_q.shape
    block = rows // BLOCKS
    even = lax.broadcasted_iota(jnp.int32, (rows, HEAD_DIM), 1) % 2 == 0
    key_all = key[...]
    value_all = value[...]
    dims_last = (((1,), (1,)), ((), ()))
    dims_first = (((0,), (0,)), ((), ()))

    def turned(values, direction):
        following = pltpu.roll(values, HEAD_DIM - 1, 1)
        preceding = pltpu.roll(values, 1, 1)
        partner = jnp.where(even, -following, preceding)
        return values * cosine[...] + direction * partner * sine[...]

    key_grad[...] = jnp.zeros_like(key_grad)
    value_grad[...] = jnp.zeros_like(value_grad)
    for head in range(columns // HEAD_DIM):
        cols = slice(head * HEAD_DIM, (head + 1) * HEAD_DIM)
        query_sum = own_q[:, cols].astype(jnp.float32) + add_q[:, cols].astype(jnp.float32)
        query_sum += adapter_scale * jnp.dot(
            low[...], up[:, cols], preferred_element_type=jnp.float32
        )
        query = turned(query_sum, 1.0).astype(jnp.bfloat16)
        grad_sum = own_g[:, cols].astype(jnp.float32) + add_g[:, cols].astype(jnp.float32)
        grad_sum += adapter_scale * jnp.dot(
            low_g[...], up_g[:, cols], preferred_element_type=jnp.float32
        )
        grad = grad_sum.astype(jnp.bfloat16)
        query_terms = []
        for index in range(BLOCKS):
            start, stop = index * block, (index + 1) * block
            query_block = query[start:stop]
            grad_block = grad[start:stop]
            key_part = key_all[:stop]
            value_part = value_all[:stop]
            scores = (
                lax.dot_general(query_block, key_part, dims_last, preferred_element_type=jnp.float32)
                * scale
            )
            row = start + lax.broadcasted_iota(jnp.int32, (block, stop), 0)
            column = lax.broadcasted_iota(jnp.int32, (block, stop), 1)
            scores = jnp.where(row >= column, scores, -jnp.inf)
            shifted = jnp.exp(scores - jnp.max(scores, axis=1, keepdims=True))
            probs = shifted * (1.0 / jnp.sum(shifted, axis=1, keepdims=True))
            weights = probs.astype(jnp.bfloat16)
            attended = jnp.dot(weights, value_part, preferred_element_type=jnp.float32).astype(
                jnp.bfloat16
            )
            attention[start:stop, cols] = attended
            prob_grad = lax.dot_general(
                grad_block, value_part, dims_last, preferred_element_type=jnp.float32
            )
            delta = jnp.sum(
                grad_block.astype(jnp.float32) * attended.astype(jnp.float32), axis=1, keepdims=True
            )
            score_grad = (probs * ((prob_grad - delta) * scale)).astype(jnp.bfloat16)
            query_terms.append(jnp.dot(score_grad, key_part, preferred_element_type=jnp.float32))
            key_grad[:stop, :] += lax.dot_general(
                score_grad, query_block, dims_first, preferred_element_type=jnp.float32
            )
            value_grad[:stop, :] += lax.dot_general(
                weights, grad_block, dims_first, preferred_element_type=jnp.float32
            )
        query_grad[:, cols] = turned(jnp.concatenate(query_terms, 0), -1.0).astype(jnp.bfloat16)


def attend(scale, *operands):
    rows, columns = operands[0].shape
    pairs = rows * rows * columns
    return pl.pallas_call(
        functools.partial(causal_heads, scale),
        out_shape=(
            jax.ShapeDtypeStruct((rows, columns), jnp.bfloat16),
            jax.ShapeDtypeStruct((rows, columns), jnp.bfloat16),
            jax.ShapeDtypeStruct((rows, HEAD_DIM), jnp.float32),
            jax.ShapeDtypeStruct((rows, HEAD_DIM), jnp.float32),
        ),
        in_specs=[pl.BlockSpec(memory_space=pltpu.VMEM)] * len(operands),
        out_specs=(pl.BlockSpec(memory_space=pltpu.VMEM),) * 4,
        compiler_params=pltpu.CompilerParams(vmem_limit_bytes=40 * 1024 * 1024),
        cost_estimate=pl.CostEstimate(
            flops=12 * pairs, bytes_accessed=16 * rows * columns, transcendentals=pairs // HEAD_DIM
        ),
    )(*operands)


def pair_sum(values, axis):
    for bit in range(lax.axis_size(axis).bit_length() - 1):
        values = values + from_partner(values, axis, bit)
    return values


def scatter_tokens(parts, axis):
    count = lax.axis_size(axis)
    index = lax.axis_index(axis)
    bits = count.bit_length() - 1
    rows = parts.shape[0] // count
    held = parts.reshape((2,) * bits + (rows, parts.shape[1]))
    for bit in range(bits):
        dim = bits - 1 - bit
        side = (index >> bit) % 2
        mine = lax.dynamic_index_in_dim(held, side, dim, keepdims=False)
        theirs = lax.dynamic_index_in_dim(held, 1 - side, dim, keepdims=False)
        received = from_partner(theirs.astype(jnp.bfloat16), axis, bit)
        held = mine.astype(jnp.float32) + received.astype(jnp.float32)
    return held


def end_streams(
    hidden,
    upstream,
    query_frozen_weight,
    key_value_frozen_weight,
    output_frozen_weight,
    adapter_down,
    query_up_map,
    key_value_up_maps,
    output_down_map,
    output_up,
):
    ffn_count = lax.axis_size("ffn")
    width_count = lax.axis_size("width")
    ffn_index = lax.axis_index("ffn")
    width_index = lax.axis_index("width")
    last = width_count - 1
    hops = [
        [(hop, hop + 1), (last - hop, last - hop - 1)] for hop in range(last)
    ]
    is_last = width_index == last
    is_end = (width_index == 0) | is_last
    hidden_full = lax.all_gather(hidden, "ffn", axis=0, tiled=True)
    upstream, hidden_full = lax.optimization_barrier((upstream, hidden_full))
    upstream_full = lax.all_gather(upstream, "ffn", axis=0, tiled=True)
    token_count = hidden_full.shape[0]
    query_cols = query_frozen_weight.shape[1]
    group_cols = query_cols // 2
    chunks = group_cols // (HEAD_DIM * CHUNK_HEADS)
    chunk_cols = group_cols // chunks
    positions = jnp.arange(token_count, dtype=jnp.int32)
    scale = 1.0 / math.sqrt(HEAD_DIM)
    down_flattened = adapter_down.reshape(3 * ADAPTER_RANK, adapter_down.shape[2])

    def to_ends(first_part, last_part):
        sent = jnp.where(width_index == 0, last_part, first_part)
        received = None
        for hop in range(last):
            if hop:
                own = jnp.where(width_index == hop, last_part, first_part)
                sent = (own.astype(jnp.float32) + received.astype(jnp.float32)).astype(jnp.bfloat16)
            received = lax.ppermute(sent, "width", hops[hop])
        return jnp.where(is_last, last_part, first_part), received

    first_hops = []

    def line_sum(own):
        total = own.astype(jnp.float32)
        received = None
        for hop in range(last):
            sent = own if hop == 0 else own + received
            received = lax.ppermute(sent, "width", hops[hop])
            total = total + received.astype(jnp.float32)
        return total

    def from_ends(own):
        first_side = own
        last_side = own
        received = own
        for hop in range(last):
            received = lax.ppermute(received, "width", hops[hop])
            if hop == 0:
                first_hops.append(received)
            first_side = jnp.where(width_index == hop + 1, received, first_side)
            last_side = jnp.where(width_index == last - 1 - hop, received, last_side)
        return first_side, last_side

    def mine(columns_of):
        half = columns_of.shape[-1] // 2
        return jnp.where(is_last, columns_of[..., half:], columns_of[..., :half])

    def product(left, right):
        return jnp.dot(left, right, preferred_element_type=jnp.float32).astype(jnp.bfloat16)

    key_value_parts = [product(hidden_full, key_value_frozen_weight[i]) for i in range(2)]
    own_kv, add_kv = to_ends(
        *[
            jnp.concatenate([part[:, side * HEAD_DIM : (side + 1) * HEAD_DIM] for part in key_value_parts], 1)
            for side in range(2)
        ]
    )
    low = line_sum(contract_last(down_flattened, hidden_full).astype(jnp.bfloat16))
    low = low.astype(jnp.bfloat16).T
    out_rank = line_sum(contract_last(output_up, upstream_full).astype(jnp.bfloat16))
    out_rank = out_rank.astype(jnp.bfloat16).T
    low_q = low[:, :ADAPTER_RANK]
    low_k = low[:, ADAPTER_RANK : 2 * ADAPTER_RANK]
    low_v = low[:, 2 * ADAPTER_RANK :]
    streams = []
    for chunk in range(chunks):
        spans = [
            slice(side * group_cols + chunk * chunk_cols, side * group_cols + (chunk + 1) * chunk_cols)
            for side in range(2)
        ]
        query_stream = to_ends(*[product(hidden_full, query_frozen_weight[:, s]) for s in spans])
        grad_stream = to_ends(
            *[contract_last(upstream_full, output_frozen_weight[s]).astype(jnp.bfloat16) for s in spans]
        )
        streams.append((query_stream, grad_stream))
    kv_sum = own_kv.astype(jnp.float32) + add_kv.astype(jnp.float32)
    key_up, value_up = mine(key_value_up_maps)
    key_state = rotate(
        kv_sum[:, :HEAD_DIM]
        + adapter_scale * jnp.dot(low_k, key_up, preferred_element_type=jnp.float32),
        positions, 0, 1.0,
    ).astype(jnp.bfloat16)
    value_state = (
        kv_sum[:, HEAD_DIM:]
        + adapter_scale * jnp.dot(low_v, value_up, preferred_element_type=jnp.float32)
    ).astype(jnp.bfloat16)
    head_dims = jnp.arange(HEAD_DIM, dtype=jnp.int32)
    frequency = jnp.exp(
        (head_dims - head_dims % 2).astype(jnp.float32) * (-math.log(rope_base) / HEAD_DIM)
    )
    angles = positions.astype(jnp.float32)[:, None] * frequency[None, :]
    cosine, sine = jnp.cos(angles), jnp.sin(angles)
    my_up = mine(query_up_map)
    my_down = mine(output_down_map)
    attentions, query_sides = [], []
    key_total = value_total = 0.0
    for chunk, ((own_q, add_q), (own_g, add_g)) in enumerate(streams):
        cols = slice(chunk * chunk_cols, (chunk + 1) * chunk_cols)
        if chunk > 1:
            add_q, first_hops[chunk - 2] = lax.optimization_barrier((add_q, first_hops[chunk - 2]))
        attention, query_grad, key_term, value_term = attend(
            scale, own_q, add_q, low_q, my_up[:, cols], own_g, add_g, out_rank, my_down[:, cols],
            key_state, value_state, cosine, sine,
        )
        attentions.append(attention)
        key_total += key_term
        value_total += value_term
        query_sides.append(from_ends(query_grad))
    attention = jnp.concatenate(attentions, 1)
    key_value_grad = jnp.concatenate(
        [
            rotate(key_total, positions, 0, -1.0).astype(jnp.bfloat16),
            value_total.astype(jnp.bfloat16),
        ],
        1,
    )
    kv_sides = from_ends(key_value_grad)
    key_grad = jnp.concatenate([side[:, :HEAD_DIM] for side in kv_sides], 1)
    value_grad = jnp.concatenate([side[:, HEAD_DIM:] for side in kv_sides], 1)
    query_grad = jnp.concatenate([sides[i] for i in range(2) for sides in query_sides], 1)

    outer_terms = jnp.where(is_end, contract_last(my_down, attention), 0.0)
    outer_rank = pair_sum(line_sum(outer_terms), "ffn").astype(jnp.bfloat16).T
    output_down_map_gradient = adapter_scale * jnp.concatenate(
        from_ends(contract_leading(out_rank, attention)), 1
    )
    output_up_map_gradient = adapter_scale * contract_leading(outer_rank, upstream_full)

    rank_terms = jnp.concatenate(
        [
            contract_last(query_up_map, query_grad),
            contract_last(key_value_up_maps[0], key_grad),
            contract_last(key_value_up_maps[1], value_grad),
        ],
        axis=0,
    )
    rank_gradient = pair_sum(rank_terms, "ffn").astype(jnp.bfloat16).T
    input_sums = []
    out_cols = query_frozen_weight.shape[0] // PIECES
    for piece in range(PIECES):
        rows = slice(piece * out_cols, (piece + 1) * out_cols)
        total = (
            contract_last(query_grad, query_frozen_weight[rows])
            + contract_last(key_grad, key_value_frozen_weight[0, rows])
            + contract_last(value_grad, key_value_frozen_weight[1, rows])
        ).astype(jnp.bfloat16)
        input_sums.append(scatter_tokens(total, "ffn"))
    own_rows = token_count // ffn_count
    rank_rows = lax.dynamic_slice_in_dim(rank_gradient, ffn_index * own_rows, own_rows, 0)
    hidden_gradient = (
        jnp.concatenate(input_sums, 1)
        + adapter_scale * jnp.dot(rank_rows, down_flattened, preferred_element_type=jnp.float32)
    ).astype(jnp.bfloat16)
    down_map_gradient = (adapter_scale * contract_leading(rank_gradient, hidden_full)).reshape(
        adapter_down.shape
    )
    query_up_map_gradient = adapter_scale * contract_leading(low_q, query_grad)
    key_value_up_maps_gradient = adapter_scale * jnp.stack(
        [contract_leading(low_k, key_grad), contract_leading(low_v, value_grad)]
    )
    return (
        hidden_gradient,
        down_map_gradient,
        query_up_map_gradient,
        key_value_up_maps_gradient,
        output_down_map_gradient,
        output_up_map_gradient,
    )


def by_shape(*arrays):
    ffn_count = lax.axis_size("ffn")
    width_count = lax.axis_size("width")
    group_cols = arrays[2].shape[1] // 2
    fits = (
        arrays[3].shape[2] == 2 * HEAD_DIM
        and width_count % 2 == 0
        and ffn_count & (ffn_count - 1) == 0
        and group_cols % (HEAD_DIM * CHUNK_HEADS) == 0
        and (arrays[0].shape[0] * ffn_count) % (BLOCKS * HEAD_DIM) == 0
        and arrays[2].shape[0] % (PIECES * HEAD_DIM) == 0
    )
    return end_streams(*arrays) if fits else shards(*arrays)


def solution(mesh):
    placed = (
        P(("groups", "ffn"), "width"),
        P(("groups", "ffn"), "width"),
        P("width", "ffn"),
        P(None, "width", "ffn"),
        P("ffn", "width"),
        P("groups", None, "width"),
        P("groups", "ffn"),
        P("groups", None, "ffn"),
        P("groups", "ffn"),
        P("groups", "width"),
    )
    return jax.shard_map(
        by_shape,
        mesh=mesh,
        in_specs=placed,
        out_specs=(
            P(("groups", "ffn"), "width"),
            P("groups", None, "width"),
            P("groups", "ffn"),
            P("groups", None, "ffn"),
            P("groups", "ffn"),
            P("groups", "width"),
        ),
        check_vma=False,
    )
```

profile of v0, /device:TPU:8, one launch (start us, length us, event | category | flops | bytes accessed | tf_op | source)
XLA Modules:
  0.0 507.9 jit_solution(10950554634980917380)
XLA Ops:
  9.7 35.5 %all-gather.3.cloned.1.call-done = bf16[1024,2048]{1,0:T(8,128)(2,1)} async-done(((bf16[256,2048]{1,0:T(8,128)(2,1)}), bf16[1024,2048]{1,0:T(8,128)(2,1)}) %all-gather.3.cloned.1.call-update) | async-done | bytes 4194320 | tf_op jit(solution)/shard_map/all_gather | solution.py:394
  45.2 3.9 convolution_convert_fusion.12
  63.4 5.1 broadcast_select_fusion.5
  69.8 4.8 broadcast_select_fusion.8
  75.9 5.8 %collective-permute-done.3 = bf16[48,1024]{0,1:T(8,128)(2,1)S(1)} collective-permute-done((bf16[48,1024]{0,1:T(8,128)(2,1)S(1)}, bf16[48,1024]{0,1:T(8,128)(2,1)S(1)}, u32[]{:S(2)}, u32[]{:S(2)}) %collective-permute-start.3) | collective-permute-done | bytes 98336 | tf_op jit(solution)/shard_map/ppermute | solution.py:423
  81.8 3.6 collective-permute-start.4
  85.3 3.3 broadcast_select_fusion.3
  90.6 4.2 collective-permute-start.5
  94.8 3.4 broadcast_select_fusion.1
  105.1 3.4 collective-permute-start.19
  111.2 4.2 collective-permute-done.27
  115.7 3.4 collective-permute-start.28
  119.1 6.9 %collective-permute-done.36 = bf16[1024,256]{1,0:T(8,128)(2,1)S(1)} collective-permute-done((bf16[1024,256]{1,0:T(8,128)(2,1)S(1)}, bf16[1024,256]{1,0:T(8,128)(2,1)S(1)}, u32[]{:S(2)}, u32[]{:S(2)}) %collective-permute-start.36) | collective-permute-done | bytes 524320 | tf_op jit(solution)/shard_map/ppermute | solution.py:413
  126.2 3.4 collective-permute-start.37
  134.3 6.2 %collective-permute-done.1 = bf16[1024,256]{1,0:T(8,128)(2,1)S(1)} collective-permute-done((bf16[1024,256]{1,0:T(8,128)(2,1)S(1)}, bf16[1024,256]{1,0:T(8,128)(2,1)S(1)}, u32[]{:S(2)}, u32[]{:S(2)}) %collective-permute-start.1) | collective-permute-done | bytes 524320 | tf_op jit(solution)/shard_map/ppermute | solution.py:413
  142.8 8.9 %collective-permute-done.28 = bf16[1024,256]{1,0:T(8,128)(2,1)S(1)} collective-permute-done((bf16[1024,256]{1,0:T(8,128)(2,1)S(1)}, bf16[1024,256]{1,0:T(8,128)(2,1)S(1)}, u32[]{:S(2)}, u32[]{:S(2)}) %collective-permute-start.28) | collective-permute-done | bytes 524320 | tf_op jit(solution)/shard_map/ppermute | solution.py:413
  154.9 4.5 collective-permute-done.37
  161.6 4.3 multiply_sine_fusion
  166.0 4.1 convolution_convert_fusion.8
  170.1 3.9 broadcast_select_fusion.4
  179.1 3.8 convolution_convert_fusion.14
  182.9 2.5 convolution_convert_fusion.4
  185.4 2.5 broadcast_select_fusion.7
  187.9 2.5 broadcast_select_fusion.2
  193.0 2.5 collective-permute-start.10
  195.5 2.5 convolution_convert_fusion
  198.1 3.2 collective-permute-done.10
  203.8 2.5 broadcast_select_fusion
  212.6 11.7 %collective-permute-done.6 = bf16[1024,256]{1,0:T(8,128)(2,1)S(1)} collective-permute-done((bf16[1024,256]{1,0:T(8,128)(2,1)S(1)}, bf16[1024,256]{1,0:T(8,128)(2,1)S(1)}, u32[]{:S(2)}, u32[]{:S(2)}) %collective-permute-start.6) | collective-permute-done | bytes 524320 | tf_op jit(solution)/shard_map/ppermute | solution.py:413
  225.8 8.5 %collective-permute-done.30 = bf16[1024,256]{1,0:T(8,128)(2,1)S(1)} collective-permute-done((bf16[1024,256]{1,0:T(8,128)(2,1)S(1)}, bf16[1024,256]{1,0:T(8,128)(2,1)S(1)}, u32[]{:S(2)}, u32[]{:S(2)}) %collective-permute-start.30) | collective-permute-done | bytes 524320 | tf_op jit(solution)/shard_map/ppermute | solution.py:413
  234.2 2.5 collective-permute-start.7
  237.0 2.9 collective-permute-done.39
  239.9 2.5 collective-permute-start.22
  242.6 8.3 %collective-permute-done.7 = bf16[1024,256]{1,0:T(8,128)(2,1)S(1)} collective-permute-done((bf16[1024,256]{1,0:T(8,128)(2,1)S(1)}, bf16[1024,256]{1,0:T(8,128)(2,1)S(1)}, u32[]{:S(2)}, u32[]{:S(2)}) %collective-permute-start.7) | collective-permute-done | bytes 524320 | tf_op jit(solution)/shard_map/ppermute | solution.py:413
  250.9 2.5 collective-permute-start.31
  253.6 6.4 %collective-permute-done.22 = bf16[1024,256]{1,0:T(8,128)(2,1)S(1)} collective-permute-done((bf16[1024,256]{1,0:T(8,128)(2,1)S(1)}, bf16[1024,256]{1,0:T(8,128)(2,1)S(1)}, u32[]{:S(2)}, u32[]{:S(2)}) %collective-permute-start.22) | collective-permute-done | bytes 524320 | tf_op jit(solution)/shard_map/ppermute | solution.py:413
  261.5 4.1 collective-permute-done.31
  269.3 4.3 collective-permute-done.8.add_g
  273.6 2.9 collective-permute-start.40
  277.6 8.6 %shard_map.145 = (bf16[1024,256]{1,0:T(8,128)(2,1)S(1)}, bf16[1024,256]{1,0:T(8,128)(2,1)S(1)}, f32[1024,128]{1,0:T(8,128)S(1)}, f32[1024,128]{1,0:T(8,128)S(1)}) custom-call(bf16[1024,256]{1,0:T(8,128)(2,1)S(1)} %copy-done.10, bf16[1024,256]{1,0:T(8,128)(2,1)S(1)} %copy-done.6, bf16[1024,16]{1,0:T(8,128)(2,1)S(1)} %bitcast.119, ...), custom_call_target="tpu_custom_call" | custom-call | flops 3221225472 | bytes 4194304 | tf_op jit(solution)/shard_map/pallas_call | solution.py:333
  286.3 2.6 collective-permute-start.32
  291.3 9.7 %shard_map.146 = (bf16[1024,256]{1,0:T(8,128)(2,1)S(1)}, bf16[1024,256]{1,0:T(8,128)(2,1)S(1)}, f32[1024,128]{1,0:T(8,128)S(1)}, f32[1024,128]{1,0:T(8,128)S(1)}) custom-call(bf16[1024,256]{1,0:T(8,128)(2,1)S(1)} %copy-done.9, bf16[1024,256]{1,0:T(8,128)(2,1)} %collective-permute-done.20.add_q, bf16[1024,16]{1,0:T(8,128)(2,1)S(1)} %bitcast.120, ...), custom_call_target="tpu_custom_call" | custom-call | flops 3221225472 | bytes 4194304 | tf_op jit(solution)/shard_map/pallas_call | solution.py:333
  302.7 6.4 %collective-permute-start.41 = (bf16[1024,256]{1,0:T(8,128)(2,1)S(1)}, bf16[1024,256]{1,0:T(8,128)(2,1)S(1)}, u32[]{:S(2)}, u32[]{:S(2)}) collective-permute-start(bf16[1024,256]{1,0:T(8,128)(2,1)S(1)} %add_convert_fusion.2), channel_id=1, source_target_pairs={{2,3},{1,0},{6,7},{5,4},{10,11},{9,8},{14,15},{13,12},{18,19},{17,... | collective-permute-start | bytes 1572872 | tf_op jit(solution)/shard_map/ppermute | solution.py:413
  309.2 3.9 collective-permute-done.24
  313.1 9.7 %shard_map.147 = (bf16[1024,256]{1,0:T(8,128)(2,1)S(1)}, bf16[1024,256]{1,0:T(8,128)(2,1)S(1)}, f32[1024,128]{1,0:T(8,128)S(1)}, f32[1024,128]{1,0:T(8,128)S(1)}) custom-call(bf16[1024,256]{1,0:T(8,128)(2,1)S(1)} %copy-done.8, bf16[1024,256]{1,0:T(8,128)(2,1)} %collective-permute-done.29.add_q, bf16[1024,16]{1,0:T(8,128)(2,1)S(1)} %bitcast.121, ...), custom_call_target="tpu_custom_call" | custom-call | flops 3221225472 | bytes 4194304 | tf_op jit(solution)/shard_map/pallas_call | solution.py:333
  324.0 9.0 %shard_map.148 = (bf16[1024,256]{1,0:T(8,128)(2,1)S(1)}, bf16[1024,256]{1,0:T(8,128)(2,1)S(1)}, f32[1024,128]{1,0:T(8,128)S(1)}, f32[1024,128]{1,0:T(8,128)S(1)}) custom-call(bf16[1024,256]{1,0:T(8,128)(2,1)S(1)} %copy-done.7, bf16[1024,256]{1,0:T(8,128)(2,1)S(1)} %collective-permute-done.38.add_q, bf16[1024,16]{1,0:T(8,128)(2,1)S(1)} %bitcast.122, ...), custom_call_target="tpu_custom_call" | custom-call | flops 3221225472 | bytes 4194304 | tf_op jit(solution)/shard_map/pallas_call | solution.py:333
  337.4 2.9 collective-permute-done.57
  340.3 2.6 collective-permute-start.58
  355.3 3.6 collective-permute-start.55
  358.9 6.1 %collective-permute-done.55 = f32[16,1024]{1,0:T(8,128)S(1)} collective-permute-done((f32[16,1024]{1,0:T(8,128)S(1)}, f32[16,1024]{1,0:T(8,128)S(1)}, u32[]{:S(2)}, u32[]{:S(2)}) %collective-permute-start.55) | collective-permute-done | bytes 65568 | tf_op jit(solution)/shard_map/ppermute | solution.py:432
  370.2 3.5 collective-permute-done.61
  376.1 3.6 collective-permute-start.46
  382.0 3.6 collective-permute-start.34
  387.5 3.2 collective-permute-done.25
  392.0 3.5 convolution_multiply_fusion.3
  395.5 6.3 %collective-permute-done.46 = bf16[1024,256]{1,0:T(8,128)(2,1)S(1)} collective-permute-done((bf16[1024,256]{1,0:T(8,128)(2,1)}, bf16[1024,256]{1,0:T(8,128)(2,1)S(1)}, u32[]{:S(2)}, u32[]{:S(2)}) %collective-permute-start.46) | collective-permute-done | bytes 524320 | tf_op jit(solution)/shard_map/ppermute | solution.py:432
  403.2 9.9 %collective-permute-done.43 = bf16[1024,256]{1,0:T(8,128)(2,1)S(1)} collective-permute-done((bf16[1024,256]{1,0:T(8,128)(2,1)}, bf16[1024,256]{1,0:T(8,128)(2,1)S(1)}, u32[]{:S(2)}, u32[]{:S(2)}) %collective-permute-start.43) | collective-permute-done | bytes 524320 | tf_op jit(solution)/shard_map/ppermute | solution.py:432
  414.4 7.7 %collective-permute-done.34 = bf16[1024,256]{1,0:T(8,128)(2,1)S(1)} collective-permute-done((bf16[1024,256]{1,0:T(8,128)(2,1)}, bf16[1024,256]{1,0:T(8,128)(2,1)S(1)}, u32[]{:S(2)}, u32[]{:S(2)}) %collective-permute-start.34) | collective-permute-done | bytes 524320 | tf_op jit(solution)/shard_map/ppermute | solution.py:432
  428.0 13.2 %collective-permute-done.35 = bf16[1024,256]{1,0:T(8,128)(2,1)S(1)} collective-permute-done((bf16[1024,256]{1,0:T(8,128)(2,1)S(1)}, bf16[1024,256]{1,0:T(8,128)(2,1)S(1)}, u32[]{:S(2)}, u32[]{:S(2)}) %collective-permute-start.35) | collective-permute-done | bytes 524320 | tf_op jit(solution)/shard_map/ppermute | solution.py:432
  450.3 4.5 fusion.2
  455.6 6.6 %fusion = f32[1024,1024]{1,0:T(8,128)S(1)} fusion(bf16[1024,2048]{1,0:T(8,128)(2,1)S(1)} %select_dynamic-update-slice_fusion, bf16[2048,2048]{1,0:T(8,128)(2,1)} %param.12), kind=kOutput, calls=%fused_computation.1 | convolution fusion | flops 4294967296 | bytes 12582912 | tf_op jit(solution)/shard_map/dot_general | solution.py:41
  468.4 5.6 %collective-permute-done.53 = f32[48,1024]{1,0:T(8,128)S(1)} collective-permute-done((f32[48,1024]{1,0:T(8,128)S(1)}, f32[48,1024]{1,0:T(8,128)S(1)}, u32[]{:S(2)}, u32[]{:S(2)}) %collective-permute-start.53) | collective-permute-done | bytes 196640 | tf_op jit(solution)/shard_map/ppermute | solution.py:24
  478.7 10.6 %collective-permute-done.49 = bf16[256,1024]{1,0:T(8,128)(2,1)S(1)} collective-permute-done((bf16[256,1024]{1,0:T(8,128)(2,1)S(1)}, bf16[256,1024]{1,0:T(8,128)(2,1)S(1)}, u32[]{:S(2)}, u32[]{:S(2)}) %collective-permute-start.49) | collective-permute-done | bytes 524320 | tf_op jit(solution)/shard_map/ppermute | solution.py:24
  489.5 9.7 %collective-permute-done.51 = bf16[256,1024]{1,0:T(8,128)(2,1)S(1)} collective-permute-done((bf16[256,1024]{1,0:T(8,128)(2,1)S(1)}, bf16[256,1024]{1,0:T(8,128)(2,1)S(1)}, u32[]{:S(2)}, u32[]{:S(2)}) %collective-permute-start.51) | collective-permute-done | bytes 524320 | tf_op jit(solution)/shard_map/ppermute | solution.py:24
  (253 shorter events, 134.0 us)
Async XLA Ops:
  7.2 38.0 %all-gather.3.cloned.1.call-start = ((), (), s32[]{:S(2)}) async-start(), calls=%async_computation | async-start | bytes 5242880 | tf_op jit(solution)/shard_map/all_gather | solution.py:394
  7.9 158.0 %all-gather.5.cloned.1.call-start = ((), (), s32[]{:S(2)}) async-start(), calls=%async_computation.1 | async-start | bytes 5242880 | tf_op jit(solution)/shard_map/all_gather | solution.py:396
  59.2 40.8 %collective-permute-start.12 = (bf16[1024,256]{1,0:T(8,128)(2,1)}, bf16[1024,256]{1,0:T(8,128)(2,1)}, u32[]{:S(2)}, u32[]{:S(2)}) collective-permute-start(bf16[1024,256]{1,0:T(8,128)(2,1)} %broadcast_select_fusion.6), channel_id=1, source_target_pairs={{0,1},{3,2},{4,5},{7,6},{8,9},{11,10},{12,13},{15,14},{16,17},{19,... | collective-permute-start | bytes 1572872 | tf_op jit(solution)/shard_map/ppermute | solution.py:413
  62.1 19.7 %collective-permute-start.3 = (bf16[48,1024]{0,1:T(8,128)(2,1)S(1)}, bf16[48,1024]{0,1:T(8,128)(2,1)S(1)}, u32[]{:S(2)}, u32[]{:S(2)}) collective-permute-start(bf16[48,1024]{0,1:T(8,128)(2,1)S(1)} %bitcast.131), channel_id=1, source_target_pairs={{0,1},{3,2},{4,5},{7,6},{8,9},{11,10},{12,13},{15,14},{16,17},{19,... | collective-permute-start | bytes 294920 | tf_op jit(solution)/shard_map/ppermute | solution.py:423
  68.4 35.4 %collective-permute-start.18 = (bf16[1024,256]{1,0:T(8,128)(2,1)}, bf16[1024,256]{1,0:T(8,128)(2,1)}, u32[]{:S(2)}, u32[]{:S(2)}) collective-permute-start(bf16[1024,256]{1,0:T(8,128)(2,1)} %get-tuple-element.58), channel_id=1, source_target_pairs={{0,1},{3,2},{4,5},{7,6},{8,9},{11,10},{12,13},{15,14},{16,17},{19,... | collective-permute-start | bytes 1572872 | tf_op jit(solution)/shard_map/ppermute | solution.py:413
  74.6 33.9 %collective-permute-start = (bf16[1024,256]{1,0:T(8,128)(2,1)S(1)}, bf16[1024,256]{1,0:T(8,128)(2,1)S(1)}, u32[]{:S(2)}, u32[]{:S(2)}) collective-permute-start(bf16[1024,256]{1,0:T(8,128)(2,1)S(1)} %get-tuple-element.62), channel_id=1, source_target_pairs={{0,1},{3,2},{4,5},{7,6},{8,9},{11,10},{12,13},{15,14},{16,17},{19,... | collective-permute-start | bytes 1572872 | tf_op jit(solution)/shard_map/ppermute | solution.py:413
  81.8 8.7 %collective-permute-start.4 = (bf16[48,1024]{0,1:T(8,128)(2,1)S(1)}, bf16[48,1024]{0,1:T(8,128)(2,1)S(1)}, u32[]{:S(2)}, u32[]{:S(2)}) collective-permute-start(bf16[48,1024]{0,1:T(8,128)(2,1)S(1)} %bitcast_add_fusion.5), channel_id=1, source_target_pairs={{1,2},{2,1},{5,6},{6,5},{9,10},{10,9},{13,14},{14,13},{17,18},{18,... | collective-permute-start | bytes 294920 | tf_op jit(solution)/shard_map/ppermute | solution.py:423
  88.7 26.8 %collective-permute-start.27 = (bf16[1024,256]{1,0:T(8,128)(2,1)S(1)}, bf16[1024,256]{1,0:T(8,128)(2,1)S(1)}, u32[]{:S(2)}, u32[]{:S(2)}) collective-permute-start(bf16[1024,256]{1,0:T(8,128)(2,1)S(1)} %get-tuple-element.54), channel_id=1, source_target_pairs={{0,1},{3,2},{4,5},{7,6},{8,9},{11,10},{12,13},{15,14},{16,17},{19,... | collective-permute-start | bytes 1572872 | tf_op jit(solution)/shard_map/ppermute | solution.py:413
  90.6 8.1 %collective-permute-start.5 = (bf16[48,1024]{0,1:T(8,128)(2,1)S(1)}, bf16[48,1024]{0,1:T(8,128)(2,1)S(1)}, u32[]{:S(2)}, u32[]{:S(2)}) collective-permute-start(bf16[48,1024]{0,1:T(8,128)(2,1)S(1)} %bitcast_add_fusion.4), channel_id=1, source_target_pairs={{2,3},{1,0},{6,7},{5,4},{10,11},{9,8},{14,15},{13,12},{18,19},{17,... | collective-permute-start | bytes 294920 | tf_op jit(solution)/shard_map/ppermute | solution.py:423
  98.6 27.3 %collective-permute-start.36 = (bf16[1024,256]{1,0:T(8,128)(2,1)S(1)}, bf16[1024,256]{1,0:T(8,128)(2,1)S(1)}, u32[]{:S(2)}, u32[]{:S(2)}) collective-permute-start(bf16[1024,256]{1,0:T(8,128)(2,1)S(1)} %get-tuple-element.50), channel_id=1, source_target_pairs={{0,1},{3,2},{4,5},{7,6},{8,9},{11,10},{12,13},{15,14},{16,17},{19,... | collective-permute-start | bytes 1572872 | tf_op jit(solution)/shard_map/ppermute | solution.py:413
  101.3 28.2 %collective-permute-start.13 = (bf16[1024,256]{1,0:T(8,128)(2,1)S(1)}, bf16[1024,256]{1,0:T(8,128)(2,1)S(1)}, u32[]{:S(2)}, u32[]{:S(2)}) collective-permute-start(bf16[1024,256]{1,0:T(8,128)(2,1)S(1)} %add_convert_fusion.15), channel_id=1, source_target_pairs={{1,2},{2,1},{5,6},{6,5},{9,10},{10,9},{13,14},{14,13},{17,18},{18,... | collective-permute-start | bytes 1572872 | tf_op jit(solution)/shard_map/ppermute | solution.py:413
  105.1 26.0 %collective-permute-start.19 = (bf16[1024,256]{1,0:T(8,128)(2,1)S(1)}, bf16[1024,256]{1,0:T(8,128)(2,1)S(1)}, u32[]{:S(2)}, u32[]{:S(2)}) collective-permute-start(bf16[1024,256]{1,0:T(8,128)(2,1)S(1)} %add_convert_fusion.13), channel_id=1, source_target_pairs={{1,2},{2,1},{5,6},{6,5},{9,10},{10,9},{13,14},{14,13},{17,18},{18,... | collective-permute-start | bytes 1572872 | tf_op jit(solution)/shard_map/ppermute | solution.py:413
  108.7 31.8 %collective-permute-start.1 = (bf16[1024,256]{1,0:T(8,128)(2,1)S(1)}, bf16[1024,256]{1,0:T(8,128)(2,1)S(1)}, u32[]{:S(2)}, u32[]{:S(2)}) collective-permute-start(bf16[1024,256]{1,0:T(8,128)(2,1)S(1)} %add_convert_fusion.19), channel_id=1, source_target_pairs={{1,2},{2,1},{5,6},{6,5},{9,10},{10,9},{13,14},{14,13},{17,18},{18,... | collective-permute-start | bytes 1572872 | tf_op jit(solution)/shard_map/ppermute | solution.py:413
  115.7 36.1 %collective-permute-start.28 = (bf16[1024,256]{1,0:T(8,128)(2,1)S(1)}, bf16[1024,256]{1,0:T(8,128)(2,1)S(1)}, u32[]{:S(2)}, u32[]{:S(2)}) collective-permute-start(bf16[1024,256]{1,0:T(8,128)(2,1)S(1)} %add_convert_fusion.9), channel_id=1, source_target_pairs={{1,2},{2,1},{5,6},{6,5},{9,10},{10,9},{13,14},{14,13},{17,18},{18,... | collective-permute-start | bytes 1572872 | tf_op jit(solution)/shard_map/ppermute | solution.py:413
  126.2 33.3 %collective-permute-start.37 = (bf16[1024,256]{1,0:T(8,128)(2,1)S(1)}, bf16[1024,256]{1,0:T(8,128)(2,1)S(1)}, u32[]{:S(2)}, u32[]{:S(2)}) collective-permute-start(bf16[1024,256]{1,0:T(8,128)(2,1)S(1)} %add_convert_fusion.5), channel_id=1, source_target_pairs={{1,2},{2,1},{5,6},{6,5},{9,10},{10,9},{13,14},{14,13},{17,18},{18,... | collective-permute-start | bytes 1572872 | tf_op jit(solution)/shard_map/ppermute | solution.py:413
  129.8 30.7 %collective-permute-start.14 = (bf16[1024,256]{1,0:T(8,128)(2,1)S(1)}, bf16[1024,256]{1,0:T(8,128)(2,1)S(1)}, u32[]{:S(2)}, u32[]{:S(2)}) collective-permute-start(bf16[1024,256]{1,0:T(8,128)(2,1)S(1)} %add_convert_fusion.14), channel_id=1, source_target_pairs={{2,3},{1,0},{6,7},{5,4},{10,11},{9,8},{14,15},{13,12},{18,19},{17,... | collective-permute-start | bytes 1572872 | tf_op jit(solution)/shard_map/ppermute | solution.py:413
  132.2 154.1 %collective-permute-start.20 = (bf16[1024,256]{1,0:T(8,128)(2,1)}, bf16[1024,256]{1,0:T(8,128)(2,1)}, u32[]{:S(2)}, u32[]{:S(2)}) collective-permute-start(bf16[1024,256]{1,0:T(8,128)(2,1)} %add_convert_fusion.12), channel_id=1, source_target_pairs={{2,3},{1,0},{6,7},{5,4},{10,11},{9,8},{14,15},{13,12},{18,19},{17,... | collective-permute-start | bytes 1572872 | tf_op jit(solution)/shard_map/ppermute | solution.py:413
  141.5 125.6 %collective-permute-start.2 = (bf16[1024,256]{1,0:T(8,128)(2,1)}, bf16[1024,256]{1,0:T(8,128)(2,1)S(1)}, u32[]{:S(2)}, u32[]{:S(2)}) collective-permute-start(bf16[1024,256]{1,0:T(8,128)(2,1)} %add_convert_fusion.18), channel_id=1, source_target_pairs={{2,3},{1,0},{6,7},{5,4},{10,11},{9,8},{14,15},{13,12},{18,19},{17,... | collective-permute-start | bytes 1572872 | tf_op jit(solution)/shard_map/ppermute | solution.py:413
  152.8 149.8 %collective-permute-start.29 = (bf16[1024,256]{1,0:T(8,128)(2,1)}, bf16[1024,256]{1,0:T(8,128)(2,1)}, u32[]{:S(2)}, u32[]{:S(2)}) collective-permute-start(bf16[1024,256]{1,0:T(8,128)(2,1)} %add_convert_fusion.8), channel_id=1, source_target_pairs={{2,3},{1,0},{6,7},{5,4},{10,11},{9,8},{14,15},{13,12},{18,19},{17,... | collective-permute-start | bytes 1572872 | tf_op jit(solution)/shard_map/ppermute | solution.py:413
  174.0 36.0 %collective-permute-start.21 = (bf16[1024,256]{1,0:T(8,128)(2,1)}, bf16[1024,256]{1,0:T(8,128)(2,1)}, u32[]{:S(2)}, u32[]{:S(2)}) collective-permute-start(bf16[1024,256]{1,0:T(8,128)(2,1)} %get-tuple-element.56), channel_id=1, source_target_pairs={{0,1},{3,2},{4,5},{7,6},{8,9},{11,10},{12,13},{15,14},{16,17},{19,... | collective-permute-start | bytes 1572872 | tf_op jit(solution)/shard_map/ppermute | solution.py:413
  177.3 14.7 %collective-permute-start.9 = (bf16[16,1024]{0,1:T(8,128)(2,1)}, bf16[16,1024]{0,1:T(8,128)(2,1)S(1)}, u32[]{:S(2)}, u32[]{:S(2)}) collective-permute-start(bf16[16,1024]{0,1:T(8,128)(2,1)} %bitcast.3), channel_id=1, source_target_pairs={{0,1},{3,2},{4,5},{7,6},{8,9},{11,10},{12,13},{15,14},{16,17},{19,... | collective-permute-start | bytes 98312 | tf_op jit(solution)/shard_map/ppermute | solution.py:423
  193.0 8.3 %collective-permute-start.10 = (bf16[16,1024]{0,1:T(8,128)(2,1)S(1)}, bf16[16,1024]{0,1:T(8,128)(2,1)S(1)}, u32[]{:S(2)}, u32[]{:S(2)}) collective-permute-start(bf16[16,1024]{0,1:T(8,128)(2,1)S(1)} %bitcast_add_fusion.3), channel_id=1, source_target_pairs={{1,2},{2,1},{5,6},{6,5},{9,10},{10,9},{13,14},{14,13},{17,18},{18,... | collective-permute-start | bytes 98312 | tf_op jit(solution)/shard_map/ppermute | solution.py:423
  202.3 5.3 %collective-permute-start.11 = (bf16[16,1024]{0,1:T(8,128)(2,1)S(1)}, bf16[16,1024]{0,1:T(8,128)(2,1)S(1)}, u32[]{:S(2)}, u32[]{:S(2)}) collective-permute-start(bf16[16,1024]{0,1:T(8,128)(2,1)S(1)} %bitcast_add_fusion.2), channel_id=1, source_target_pairs={{2,3},{1,0},{6,7},{5,4},{10,11},{9,8},{14,15},{13,12},{18,19},{17,... | collective-permute-start | bytes 98312 | tf_op jit(solution)/shard_map/ppermute | solution.py:423
  207.6 16.7 %collective-permute-start.6 = (bf16[1024,256]{1,0:T(8,128)(2,1)S(1)}, bf16[1024,256]{1,0:T(8,128)(2,1)S(1)}, u32[]{:S(2)}, u32[]{:S(2)}) collective-permute-start(bf16[1024,256]{1,0:T(8,128)(2,1)S(1)} %get-tuple-element.60), channel_id=1, source_target_pairs={{0,1},{3,2},{4,5},{7,6},{8,9},{11,10},{12,13},{15,14},{16,17},{19,... | collective-permute-start | bytes 1572872 | tf_op jit(solution)/shard_map/ppermute | solution.py:413
  210.0 24.2 %collective-permute-start.30 = (bf16[1024,256]{1,0:T(8,128)(2,1)S(1)}, bf16[1024,256]{1,0:T(8,128)(2,1)S(1)}, u32[]{:S(2)}, u32[]{:S(2)}) collective-permute-start(bf16[1024,256]{1,0:T(8,128)(2,1)S(1)} %get-tuple-element.52), channel_id=1, source_target_pairs={{0,1},{3,2},{4,5},{7,6},{8,9},{11,10},{12,13},{15,14},{16,17},{19,... | collective-permute-start | bytes 1572872 | tf_op jit(solution)/shard_map/ppermute | solution.py:413
  224.3 15.6 %collective-permute-start.39 = (bf16[1024,256]{1,0:T(8,128)(2,1)S(1)}, bf16[1024,256]{1,0:T(8,128)(2,1)S(1)}, u32[]{:S(2)}, u32[]{:S(2)}) collective-permute-start(bf16[1024,256]{1,0:T(8,128)(2,1)S(1)} %get-tuple-element.48), channel_id=1, source_target_pairs={{0,1},{3,2},{4,5},{7,6},{8,9},{11,10},{12,13},{15,14},{16,17},{19,... | collective-permute-start | bytes 1572872 | tf_op jit(solution)/shard_map/ppermute | solution.py:413
  234.2 16.7 %collective-permute-start.7 = (bf16[1024,256]{1,0:T(8,128)(2,1)S(1)}, bf16[1024,256]{1,0:T(8,128)(2,1)S(1)}, u32[]{:S(2)}, u32[]{:S(2)}) collective-permute-start(bf16[1024,256]{1,0:T(8,128)(2,1)S(1)} %add_convert_fusion.17), channel_id=1, source_target_pairs={{1,2},{2,1},{5,6},{6,5},{9,10},{10,9},{13,14},{14,13},{17,18},{18,... | collective-permute-start | bytes 1572872 | tf_op jit(solution)/shard_map/ppermute | solution.py:413
  239.9 20.2 %collective-permute-start.22 = (bf16[1024,256]{1,0:T(8,128)(2,1)S(1)}, bf16[1024,256]{1,0:T(8,128)(2,1)S(1)}, u32[]{:S(2)}, u32[]{:S(2)}) collective-permute-start(bf16[1024,256]{1,0:T(8,128)(2,1)S(1)} %add_convert_fusion.11), channel_id=1, source_target_pairs={{1,2},{2,1},{5,6},{6,5},{9,10},{10,9},{13,14},{14,13},{17,18},{18,... | collective-permute-start | bytes 1572872 | tf_op jit(solution)/shard_map/ppermute | solution.py:413
  250.9 14.7 %collective-permute-start.31 = (bf16[1024,256]{1,0:T(8,128)(2,1)S(1)}, bf16[1024,256]{1,0:T(8,128)(2,1)S(1)}, u32[]{:S(2)}, u32[]{:S(2)}) collective-permute-start(bf16[1024,256]{1,0:T(8,128)(2,1)S(1)} %add_convert_fusion.7), channel_id=1, source_target_pairs={{1,2},{2,1},{5,6},{6,5},{9,10},{10,9},{13,14},{14,13},{17,18},{18,... | collective-permute-start | bytes 1572872 | tf_op jit(solution)/shard_map/ppermute | solution.py:413
  260.0 13.6 %collective-permute-start.8 = (bf16[1024,256]{1,0:T(8,128)(2,1)S(1)}, bf16[1024,256]{1,0:T(8,128)(2,1)S(1)}, u32[]{:S(2)}, u32[]{:S(2)}) collective-permute-start(bf16[1024,256]{1,0:T(8,128)(2,1)S(1)} %add_convert_fusion.16), channel_id=1, source_target_pairs={{2,3},{1,0},{6,7},{5,4},{10,11},{9,8},{14,15},{13,12},{18,19},{17,... | collective-permute-start | bytes 1572872 | tf_op jit(solution)/shard_map/ppermute | solution.py:413
  265.6 23.2 %collective-permute-start.23 = (bf16[1024,256]{1,0:T(8,128)(2,1)S(1)}, bf16[1024,256]{1,0:T(8,128)(2,1)S(1)}, u32[]{:S(2)}, u32[]{:S(2)}) collective-permute-start(bf16[1024,256]{1,0:T(8,128)(2,1)S(1)} %add_convert_fusion.10), channel_id=1, source_target_pairs={{2,3},{1,0},{6,7},{5,4},{10,11},{9,8},{14,15},{13,12},{18,19},{17,... | collective-permute-start | bytes 1572872 | tf_op jit(solution)/shard_map/ppermute | solution.py:413
  268.0 41.2 %collective-permute-start.38 = (bf16[1024,256]{1,0:T(8,128)(2,1)S(1)}, bf16[1024,256]{1,0:T(8,128)(2,1)S(1)}, u32[]{:S(2)}, u32[]{:S(2)}) collective-permute-start(bf16[1024,256]{1,0:T(8,128)(2,1)S(1)} %copy-done.25), channel_id=1, source_target_pairs={{2,3},{1,0},{6,7},{5,4},{10,11},{9,8},{14,15},{13,12},{18,19},{17,... | collective-permute-start | bytes 1572872 | tf_op jit(solution)/shard_map/ppermute | solution.py:413
  273.6 27.4 %collective-permute-start.40 = (bf16[1024,256]{1,0:T(8,128)(2,1)S(1)}, bf16[1024,256]{1,0:T(8,128)(2,1)S(1)}, u32[]{:S(2)}, u32[]{:S(2)}) collective-permute-start(bf16[1024,256]{1,0:T(8,128)(2,1)S(1)} %add_convert_fusion.3), channel_id=1, source_target_pairs={{1,2},{2,1},{5,6},{6,5},{9,10},{10,9},{13,14},{14,13},{17,18},{18,... | collective-permute-start | bytes 1572872 | tf_op jit(solution)/shard_map/ppermute | solution.py:413
  286.3 26.8 %collective-permute-start.32 = (bf16[1024,256]{1,0:T(8,128)(2,1)S(1)}, bf16[1024,256]{1,0:T(8,128)(2,1)S(1)}, u32[]{:S(2)}, u32[]{:S(2)}) collective-permute-start(bf16[1024,256]{1,0:T(8,128)(2,1)S(1)} %add_convert_fusion.6), channel_id=1, source_target_pairs={{2,3},{1,0},{6,7},{5,4},{10,11},{9,8},{14,15},{13,12},{18,19},{17,... | collective-permute-start | bytes 1572872 | tf_op jit(solution)/shard_map/ppermute | solution.py:413
  288.8 20.3 %collective-permute-start.15 = (bf16[1024,256]{1,0:T(8,128)(2,1)S(1)}, bf16[1024,256]{1,0:T(8,128)(2,1)}, u32[]{:S(2)}, u32[]{:S(2)}) collective-permute-start(bf16[1024,256]{1,0:T(8,128)(2,1)S(1)} %get-tuple-element.28), channel_id=1, source_target_pairs={{0,1},{3,2},{4,5},{7,6},{8,9},{11,10},{12,13},{15,14},{16,17},{19,... | collective-permute-start | bytes 1572872 | tf_op jit(solution)/shard_map/ppermute | solution.py:432
  301.0 12.1 %collective-permute-start.24 = (bf16[1024,256]{1,0:T(8,128)(2,1)S(1)}, bf16[1024,256]{1,0:T(8,128)(2,1)}, u32[]{:S(2)}, u32[]{:S(2)}) collective-permute-start(bf16[1024,256]{1,0:T(8,128)(2,1)S(1)} %get-tuple-element.29), channel_id=1, source_target_pairs={{0,1},{3,2},{4,5},{7,6},{8,9},{11,10},{12,13},{15,14},{16,17},{19,... | collective-permute-start | bytes 1572872 | tf_op jit(solution)/shard_map/ppermute | solution.py:432
  302.7 20.2 %collective-permute-start.41 = (bf16[1024,256]{1,0:T(8,128)(2,1)S(1)}, bf16[1024,256]{1,0:T(8,128)(2,1)S(1)}, u32[]{:S(2)}, u32[]{:S(2)}) collective-permute-start(bf16[1024,256]{1,0:T(8,128)(2,1)S(1)} %add_convert_fusion.2), channel_id=1, source_target_pairs={{2,3},{1,0},{6,7},{5,4},{10,11},{9,8},{14,15},{13,12},{18,19},{17,... | collective-permute-start | bytes 1572872 | tf_op jit(solution)/shard_map/ppermute | solution.py:413
  334.1 6.2 %collective-permute-start.57 = (f32[16,1024]{1,0:T(8,128)S(1)}, f32[16,1024]{1,0:T(8,128)S(1)}, u32[]{:S(2)}, u32[]{:S(2)}) collective-permute-start(f32[16,1024]{1,0:T(8,128)S(1)} %convolution_select_fusion), channel_id=1, source_target_pairs={{0,1},{3,2},{4,5},{7,6},{8,9},{11,10},{12,13},{15,14},{16,17},{19,... | collective-permute-start | bytes 196616 | tf_op jit(solution)/shard_map/ppermute | solution.py:423
  335.4 17.5 %collective-permute-start.54 = (f32[16,1024]{1,0:T(8,128)S(1)}, f32[16,1024]{1,0:T(8,128)S(1)}, u32[]{:S(2)}, u32[]{:S(2)}) collective-permute-start(f32[16,1024]{1,0:T(8,128)S(1)} %fusion.82), channel_id=1, source_target_pairs={{0,1},{3,2},{4,5},{7,6},{8,9},{11,10},{12,13},{15,14},{16,17},{19,... | collective-permute-start | bytes 196616 | tf_op jit(solution)/shard_map/ppermute | solution.py:432
  340.3 6.6 %collective-permute-start.58 = (f32[16,1024]{1,0:T(8,128)S(1)}, f32[16,1024]{1,0:T(8,128)S(1)}, u32[]{:S(2)}, u32[]{:S(2)}) collective-permute-start(f32[16,1024]{1,0:T(8,128)S(1)} %add.335), channel_id=1, source_target_pairs={{1,2},{2,1},{5,6},{6,5},{9,10},{10,9},{13,14},{14,13},{17,18},{18,... | collective-permute-start | bytes 196616 | tf_op jit(solution)/shard_map/ppermute | solution.py:423
  346.9 8.4 %collective-permute-start.59 = (f32[16,1024]{1,0:T(8,128)S(1)}, f32[16,1024]{1,0:T(8,128)S(1)}, u32[]{:S(2)}, u32[]{:S(2)}) collective-permute-start(f32[16,1024]{1,0:T(8,128)S(1)} %add.337), channel_id=1, source_target_pairs={{2,3},{1,0},{6,7},{5,4},{10,11},{9,8},{14,15},{13,12},{18,19},{17,... | collective-permute-start | bytes 196616 | tf_op jit(solution)/shard_map/ppermute | solution.py:423
  349.1 27.0 %collective-permute-start.45 = (bf16[1024,256]{1,0:T(8,128)(2,1)}, bf16[1024,256]{1,0:T(8,128)(2,1)}, u32[]{:S(2)}, u32[]{:S(2)}) collective-permute-start(bf16[1024,256]{1,0:T(8,128)(2,1)} %pad_maximum_fusion.2), channel_id=1, source_target_pairs={{0,1},{3,2},{4,5},{7,6},{8,9},{11,10},{12,13},{15,14},{16,17},{19,... | collective-permute-start | bytes 1572872 | tf_op jit(solution)/shard_map/ppermute | solution.py:432
  350.4 29.3 %collective-permute-start.42 = (bf16[1024,256]{1,0:T(8,128)(2,1)S(1)}, bf16[1024,256]{1,0:T(8,128)(2,1)}, u32[]{:S(2)}, u32[]{:S(2)}) collective-permute-start(bf16[1024,256]{1,0:T(8,128)(2,1)S(1)} %get-tuple-element.33), channel_id=1, source_target_pairs={{0,1},{3,2},{4,5},{7,6},{8,9},{11,10},{12,13},{15,14},{16,17},{19,... | collective-permute-start | bytes 1572872 | tf_op jit(solution)/shard_map/ppermute | solution.py:432
  351.7 30.3 %collective-permute-start.33 = (bf16[1024,256]{1,0:T(8,128)(2,1)S(1)}, bf16[1024,256]{1,0:T(8,128)(2,1)}, u32[]{:S(2)}, u32[]{:S(2)}) collective-permute-start(bf16[1024,256]{1,0:T(8,128)(2,1)S(1)} %get-tuple-element.31), channel_id=1, source_target_pairs={{0,1},{3,2},{4,5},{7,6},{8,9},{11,10},{12,13},{15,14},{16,17},{19,... | collective-permute-start | bytes 1572872 | tf_op jit(solution)/shard_map/ppermute | solution.py:432
  353.0 32.5 %collective-permute-start.16 = (bf16[1024,256]{1,0:T(8,128)(2,1)}, bf16[1024,256]{1,0:T(8,128)(2,1)}, u32[]{:S(2)}, u32[]{:S(2)}) collective-permute-start(bf16[1024,256]{1,0:T(8,128)(2,1)} %collective-permute-done.15), channel_id=1, source_target_pairs={{1,2},{2,1},{5,6},{6,5},{9,10},{10,9},{13,14},{14,13},{17,18},{18,... | collective-permute-start | bytes 1572872 | tf_op jit(solution)/shard_map/ppermute | solution.py:432
  355.3 9.7 %collective-permute-start.55 = (f32[16,1024]{1,0:T(8,128)S(1)}, f32[16,1024]{1,0:T(8,128)S(1)}, u32[]{:S(2)}, u32[]{:S(2)}) collective-permute-start(f32[16,1024]{1,0:T(8,128)S(1)} %collective-permute-done.54), channel_id=1, source_target_pairs={{1,2},{2,1},{5,6},{6,5},{9,10},{10,9},{13,14},{14,13},{17,18},{18,... | collective-permute-start | bytes 196616 | tf_op jit(solution)/shard_map/ppermute | solution.py:432
  365.0 1.3 collective-permute-start.60
  366.2 3.2 collective-permute-start.56
  369.4 4.3 collective-permute-start.61
  373.7 17.0 %collective-permute-start.25 = (bf16[1024,256]{1,0:T(8,128)(2,1)}, bf16[1024,256]{1,0:T(8,128)(2,1)}, u32[]{:S(2)}, u32[]{:S(2)}) collective-permute-start(bf16[1024,256]{1,0:T(8,128)(2,1)} %collective-permute-done.24), channel_id=1, source_target_pairs={{1,2},{2,1},{5,6},{6,5},{9,10},{10,9},{13,14},{14,13},{17,18},{18,... | collective-permute-start | bytes 1572872 | tf_op jit(solution)/shard_map/ppermute | solution.py:432
  376.1 25.8 %collective-permute-start.46 = (bf16[1024,256]{1,0:T(8,128)(2,1)}, bf16[1024,256]{1,0:T(8,128)(2,1)S(1)}, u32[]{:S(2)}, u32[]{:S(2)}) collective-permute-start(bf16[1024,256]{1,0:T(8,128)(2,1)} %collective-permute-done.45), channel_id=1, source_target_pairs={{1,2},{2,1},{5,6},{6,5},{9,10},{10,9},{13,14},{14,13},{17,18},{18,... | collective-permute-start | bytes 1572872 | tf_op jit(solution)/shard_map/ppermute | solution.py:432
  379.6 33.4 %collective-permute-start.43 = (bf16[1024,256]{1,0:T(8,128)(2,1)}, bf16[1024,256]{1,0:T(8,128)(2,1)S(1)}, u32[]{:S(2)}, u32[]{:S(2)}) collective-permute-start(bf16[1024,256]{1,0:T(8,128)(2,1)} %collective-permute-done.42), channel_id=1, source_target_pairs={{1,2},{2,1},{5,6},{6,5},{9,10},{10,9},{13,14},{14,13},{17,18},{18,... | collective-permute-start | bytes 1572872 | tf_op jit(solution)/shard_map/ppermute | solution.py:432
  382.0 40.2 %collective-permute-start.34 = (bf16[1024,256]{1,0:T(8,128)(2,1)}, bf16[1024,256]{1,0:T(8,128)(2,1)S(1)}, u32[]{:S(2)}, u32[]{:S(2)}) collective-permute-start(bf16[1024,256]{1,0:T(8,128)(2,1)} %collective-permute-done.33), channel_id=1, source_target_pairs={{1,2},{2,1},{5,6},{6,5},{9,10},{10,9},{13,14},{14,13},{17,18},{18,... | collective-permute-start | bytes 1572872 | tf_op jit(solution)/shard_map/ppermute | solution.py:432
  385.5 38.1 %collective-permute-start.17 = (bf16[1024,256]{1,0:T(8,128)(2,1)}, bf16[1024,256]{1,0:T(8,128)(2,1)S(1)}, u32[]{:S(2)}, u32[]{:S(2)}) collective-permute-start(bf16[1024,256]{1,0:T(8,128)(2,1)} %collective-permute-done.16), channel_id=1, source_target_pairs={{2,3},{1,0},{6,7},{5,4},{10,11},{9,8},{14,15},{13,12},{18,19},{17,... | collective-permute-start | bytes 1572872 | tf_op jit(solution)/shard_map/ppermute | solution.py:432
  390.7 34.2 %collective-permute-start.26 = (bf16[1024,256]{1,0:T(8,128)(2,1)}, bf16[1024,256]{1,0:T(8,128)(2,1)S(1)}, u32[]{:S(2)}, u32[]{:S(2)}) collective-permute-start(bf16[1024,256]{1,0:T(8,128)(2,1)} %collective-permute-done.25), channel_id=1, source_target_pairs={{2,3},{1,0},{6,7},{5,4},{10,11},{9,8},{14,15},{13,12},{18,19},{17,... | collective-permute-start | bytes 1572872 | tf_op jit(solution)/shard_map/ppermute | solution.py:432
  401.8 24.5 %collective-permute-start.47 = (bf16[1024,256]{1,0:T(8,128)(2,1)S(1)}, bf16[1024,256]{1,0:T(8,128)(2,1)S(1)}, u32[]{:S(2)}, u32[]{:S(2)}) collective-permute-start(bf16[1024,256]{1,0:T(8,128)(2,1)S(1)} %collective-permute-done.46), channel_id=1, source_target_pairs={{2,3},{1,0},{6,7},{5,4},{10,11},{9,8},{14,15},{13,12},{18,19},{17,... | collective-permute-start | bytes 1572872 | tf_op jit(solution)/shard_map/ppermute | solution.py:432
  413.1 30.5 %collective-permute-start.44 = (bf16[1024,256]{1,0:T(8,128)(2,1)S(1)}, bf16[1024,256]{1,0:T(8,128)(2,1)S(1)}, u32[]{:S(2)}, u32[]{:S(2)}) collective-permute-start(bf16[1024,256]{1,0:T(8,128)(2,1)S(1)} %collective-permute-done.43), channel_id=1, source_target_pairs={{2,3},{1,0},{6,7},{5,4},{10,11},{9,8},{14,15},{13,12},{18,19},{17,... | collective-permute-start | bytes 1572872 | tf_op jit(solution)/shard_map/ppermute | solution.py:432
  422.1 19.1 %collective-permute-start.35 = (bf16[1024,256]{1,0:T(8,128)(2,1)S(1)}, bf16[1024,256]{1,0:T(8,128)(2,1)S(1)}, u32[]{:S(2)}, u32[]{:S(2)}) collective-permute-start(bf16[1024,256]{1,0:T(8,128)(2,1)S(1)} %collective-permute-done.34), channel_id=1, source_target_pairs={{2,3},{1,0},{6,7},{5,4},{10,11},{9,8},{14,15},{13,12},{18,19},{17,... | collective-permute-start | bytes 1572872 | tf_op jit(solution)/shard_map/ppermute | solution.py:432
  463.8 2.7 collective-permute-start.52
  464.7 9.2 %collective-permute-start.48 = (bf16[2,256,1024]{2,1,0:T(8,128)(2,1)S(1)}, bf16[2,256,1024]{2,1,0:T(8,128)(2,1)S(1)}, u32[]{:S(2)}, u32[]{:S(2)}) collective-permute-start(bf16[2,256,1024]{2,1,0:T(8,128)(2,1)S(1)} %dynamic-slice_bitcast_fusion.1), channel_id=1, source_target_pairs={{0,4},{4,0},{8,12},{12,8},{1,5},{5,1},{9,13},{13,9},{2,6},{6,2},{1... | collective-permute-start | bytes 3145736 | tf_op jit(solution)/shard_map/ppermute | solution.py:24
  466.1 9.2 %collective-permute-start.50 = (bf16[2,256,1024]{2,1,0:T(8,128)(2,1)S(1)}, bf16[2,256,1024]{2,1,0:T(8,128)(2,1)S(1)}, u32[]{:S(2)}, u32[]{:S(2)}) collective-permute-start(bf16[2,256,1024]{2,1,0:T(8,128)(2,1)S(1)} %dynamic-slice_bitcast_fusion), channel_id=1, source_target_pairs={{0,4},{4,0},{8,12},{12,8},{1,5},{5,1},{9,13},{13,9},{2,6},{6,2},{1... | collective-permute-start | bytes 3145736 | tf_op jit(solution)/shard_map/ppermute | solution.py:24
  466.6 7.4 %collective-permute-start.53 = (f32[48,1024]{1,0:T(8,128)S(1)}, f32[48,1024]{1,0:T(8,128)S(1)}, u32[]{:S(2)}, u32[]{:S(2)}) collective-permute-start(f32[48,1024]{1,0:T(8,128)S(1)} %fusion.71), channel_id=1, source_target_pairs={{0,8},{4,12},{8,0},{12,4},{1,9},{5,13},{9,1},{13,5},{2,10},{6,14},... | collective-permute-start | bytes 589832 | tf_op jit(solution)/shard_map/ppermute | solution.py:24
  474.5 14.9 %collective-permute-start.49 = (bf16[256,1024]{1,0:T(8,128)(2,1)S(1)}, bf16[256,1024]{1,0:T(8,128)(2,1)S(1)}, u32[]{:S(2)}, u32[]{:S(2)}) collective-permute-start(bf16[256,1024]{1,0:T(8,128)(2,1)S(1)} %fusion.33), channel_id=1, source_target_pairs={{0,8},{4,12},{8,0},{12,4},{1,9},{5,13},{9,1},{13,5},{2,10},{6,14},... | collective-permute-start | bytes 1572872 | tf_op jit(solution)/shard_map/ppermute | solution.py:24
  475.8 23.5 %collective-permute-start.51 = (bf16[256,1024]{1,0:T(8,128)(2,1)S(1)}, bf16[256,1024]{1,0:T(8,128)(2,1)S(1)}, u32[]{:S(2)}, u32[]{:S(2)}) collective-permute-start(bf16[256,1024]{1,0:T(8,128)(2,1)S(1)} %fusion.34), channel_id=1, source_target_pairs={{0,8},{4,12},{8,0},{12,4},{1,9},{5,13},{9,1},{13,5},{2,10},{6,14},... | collective-permute-start | bytes 1572872 | tf_op jit(solution)/shard_map/ppermute | solution.py:24
  (32 other events, 607.1 us)
Sparse Core Ops, SparseCore 0:
  9.5 35.5 all-gather.2
  69.9 37.2 all-gather.4
where the time goes:
time: 518 us; the launch traced here: 508 us
  waiting for transfers between devices  214 us (41%)
  starting transfers between devices  115 us (22%)
  matrix products  81.1 us (16%)
  other arithmetic  37 us (7%)
  Pallas kernels  37 us (7%)
  between operations  15.9 us (3%)
  local copies, waits for them, and re-layouts  8.31 us (2%)
    ppermute x27, waiting for transfers between devices, to_ends(): received = lax.ppermute(sent, 'width', hops[hop])  76.9 us
    ppermute x27, starting transfers between devices, to_ends(): received = lax.ppermute(sent, 'width', hops[hop])  56.8 us
    ppermute x18, waiting for transfers between devices, from_ends(): received = lax.ppermute(received, 'width', hops[hop])  52.3 us
    dot_general x20, matrix products, contract_last(): lax.dot_general(left_side, right_side, (((1,), (1,)), ((), ())), preferre...  43.3 us
    pallas_call x4, Pallas kernels, attend(): pl.pallas_call(functools.partial(causal_heads, scale), out_shape=(jax.Sha...  37 us
    all_gather x1, waiting for transfers between devices, end_streams(): hidden_full = lax.all_gather(hidden, 'ffn', axis=0, tiled=True)  35.5 us
    ppermute x18, starting transfers between devices, from_ends(): received = lax.ppermute(received, 'width', hops[hop])  33.6 us
    ppermute x8, waiting for transfers between devices, from_partner(): lax.ppermute(array, axis, [(i, i ^ 1 << bit) for i in range(lax.axis_size...  30.7 us
  transfers between devices with their start and end apart: 64, of which 34 were waited for; matrix products, arithmetic and copies ran while one was open for 17% of the time, Pallas kernels for 6%

commit v1 on v0

v1 whole, which is shorter than its diff:
```python
import functools
import math

import jax
import jax.numpy as jnp
import numpy as np
from jax import lax
from jax.experimental import pallas as pl
from jax.experimental.pallas import tpu as pltpu
from jax.sharding import PartitionSpec as P

KV_HEADS = 8
HEAD_DIM = 128
ADAPTER_RANK = 16
CHUNK_HEADS = 2
BLOCKS = 4
LAG = 3
BACK_LAG = 2
MESH = pl.DeviceIdType.MESH
LAST = (((1,), (1,)), ((), ()))
FIRST = (((0,), (0,)), ((), ()))


adapter_scale = 2.0
rope_base = 500000.0


def from_partner(array, axis, bit):
    return lax.ppermute(array, axis, [(i, i ^ 1 << bit) for i in range(lax.axis_size(axis))])


def rotate(values, positions, first_dim, direction):
    columns = values.shape[1]
    head_dims = (first_dim + jnp.arange(columns, dtype=jnp.int32)) % HEAD_DIM
    pair_dims = head_dims - head_dims % 2
    frequency = jnp.exp(pair_dims.astype(jnp.float32) * (-math.log(rope_base) / HEAD_DIM))
    angles = positions.astype(jnp.float32)[:, None] * frequency[None, :]
    is_even = head_dims % 2 == 0
    following = jnp.roll(values, -1, axis=1)
    preceding = jnp.roll(values, 1, axis=1)
    partner = jnp.where(is_even[None, :], -following, preceding)
    return values * jnp.cos(angles) + direction * partner * jnp.sin(angles)


def contract_last(left_side, right_side):
    return lax.dot_general(
        left_side, right_side, (((1,), (1,)), ((), ())), preferred_element_type=jnp.float32
    )


def contract_leading(left_side, right_side):
    return lax.dot_general(
        left_side, right_side, (((0,), (0,)), ((), ())), preferred_element_type=jnp.float32
    )


def shards(
    hidden,
    upstream,
    query_frozen_weight,
    key_value_frozen_weight,
    output_frozen_weight,
    adapter_down,
    query_up_map,
    key_value_up_maps,
    output_down_map,
    output_up,
):
    ffn_count = lax.axis_size("ffn")
    width_count = lax.axis_size("width")
    ffn_index = lax.axis_index("ffn")
    width_index = lax.axis_index("width")
    hidden_rows_full, upstream_gradient_full = (
        lax.all_gather(hidden, "ffn", axis=0, tiled=True),
        lax.all_gather(upstream, "ffn", axis=0, tiled=True),
    )
    token_count = hidden_rows_full.shape[0]
    query_rows = token_count // width_count
    query_cols = query_frozen_weight.shape[1]
    key_cols = key_value_frozen_weight.shape[2]
    row_start = width_index * query_rows
    positions = jnp.arange(token_count, dtype=jnp.int32)
    row_positions = row_start + jnp.arange(query_rows, dtype=jnp.int32)
    query_offset = ffn_index * query_cols
    key_offset = ffn_index * key_cols
    score_scale = 1.0 / math.sqrt(HEAD_DIM)
    down_flattened = adapter_down.reshape(3 * ADAPTER_RANK, adapter_down.shape[2])
    paired = ffn_count > KV_HEADS
    parity = ffn_index % 2
    rank_terms = contract_last(hidden_rows_full, down_flattened)
    upstream_terms = contract_last(upstream_gradient_full, output_up)
    rank_sum, upstream_sum = lax.psum((rank_terms, upstream_terms), "width")
    reduced_hidden = rank_sum.astype(jnp.bfloat16)
    output_reduced = upstream_sum.astype(jnp.bfloat16)
    low_rows = lax.dynamic_slice_in_dim(reduced_hidden, row_start, query_rows, 0)
    output_token_rows = lax.dynamic_slice_in_dim(output_reduced, row_start, query_rows, 0)
    query_part = jnp.dot(hidden_rows_full, query_frozen_weight, preferred_element_type=jnp.float32)
    query_gradient_summed = lax.psum_scatter(
        query_part.astype(jnp.bfloat16), "width", scatter_dimension=0, tiled=True
    ).astype(jnp.float32)
    query_projected = query_gradient_summed + adapter_scale * jnp.dot(
        low_rows[:, :ADAPTER_RANK], query_up_map, preferred_element_type=jnp.float32
    )
    query_states = rotate(query_projected, row_positions, query_offset, 1.0).astype(jnp.bfloat16)
    key_part = jnp.dot(
        hidden_rows_full, key_value_frozen_weight[0], preferred_element_type=jnp.float32
    )
    value_part = jnp.dot(
        hidden_rows_full, key_value_frozen_weight[1], preferred_element_type=jnp.float32
    )
    key_gradient_summed, value_gradient_summed = (
        lax.psum_scatter(
            key_part.astype(jnp.bfloat16), "width", scatter_dimension=0, tiled=True
        ).astype(jnp.float32),
        lax.psum_scatter(
            value_part.astype(jnp.bfloat16), "width", scatter_dimension=0, tiled=True
        ).astype(jnp.float32),
    )
    key_projected = key_gradient_summed + adapter_scale * jnp.dot(
        low_rows[:, ADAPTER_RANK : 2 * ADAPTER_RANK],
        key_value_up_maps[0],
        preferred_element_type=jnp.float32,
    )
    value_projected = value_gradient_summed + adapter_scale * jnp.dot(
        low_rows[:, 2 * ADAPTER_RANK :], key_value_up_maps[1], preferred_element_type=jnp.float32
    )
    key_block = rotate(key_projected, row_positions, key_offset, 1.0).astype(jnp.bfloat16)
    value_block = value_projected.astype(jnp.bfloat16)
    key_states, value_state_rows = (
        lax.all_gather(key_block, "width", axis=0, tiled=True),
        lax.all_gather(value_block, "width", axis=0, tiled=True),
    )
    if paired:
        other_key, other_value = from_partner((key_states, value_state_rows), "ffn", 0)
        key_states = jnp.where(
            parity == 0,
            jnp.concatenate([key_states, other_key], 1),
            jnp.concatenate([other_key, key_states], 1),
        )
        value_state_rows = jnp.where(
            parity == 0,
            jnp.concatenate([value_state_rows, other_value], 1),
            jnp.concatenate([other_value, value_state_rows], 1),
        )
    local_heads = query_cols // HEAD_DIM
    local_groups = key_states.shape[1] // HEAD_DIM
    group_size = local_heads // local_groups
    query_four = query_states.reshape(query_rows, local_groups, group_size, HEAD_DIM)
    key_three = key_states.reshape(token_count, local_groups, HEAD_DIM)
    value_three = value_state_rows.reshape(token_count, local_groups, HEAD_DIM)
    causal = row_positions[:, None] >= positions[None, :]
    scores = (
        jnp.einsum("qkgd,skd->kgqs", query_four, key_three, preferred_element_type=jnp.float32)
        * score_scale
    )
    scores = jnp.where(causal[None, None, :, :], scores, -jnp.inf)
    shifted = jnp.exp(scores - jnp.max(scores, axis=-1, keepdims=True))
    probs = shifted / jnp.sum(shifted, axis=-1, keepdims=True)
    prob_weights = probs.astype(jnp.bfloat16)
    attention_four = jnp.einsum(
        "kgqs,skd->qkgd", prob_weights, value_three, preferred_element_type=jnp.float32
    ).astype(jnp.bfloat16)
    attention_output = attention_four.reshape(query_rows, query_cols)
    out_part = contract_last(upstream_gradient_full, output_frozen_weight)
    output_gradient_summed = lax.psum_scatter(
        out_part.astype(jnp.bfloat16), "width", scatter_dimension=0, tiled=True
    ).astype(jnp.float32)
    attention_output_gradient = (
        output_gradient_summed
        + adapter_scale
        * jnp.dot(output_token_rows, output_down_map, preferred_element_type=jnp.float32)
    ).astype(jnp.bfloat16)
    grad_four = attention_output_gradient.reshape(query_rows, local_groups, group_size, HEAD_DIM)
    prob_grad = jnp.einsum(
        "qkgd,skd->kgqs", grad_four, value_three, preferred_element_type=jnp.float32
    )
    delta = jnp.einsum(
        "qkgd,qkgd->kgq", grad_four, attention_four, preferred_element_type=jnp.float32
    )
    score_grad = (probs * (prob_grad - delta[:, :, :, None]) * score_scale).astype(jnp.bfloat16)
    query_rot_grad = jnp.einsum(
        "kgqs,skd->qkgd", score_grad, key_three, preferred_element_type=jnp.float32
    ).reshape(query_rows, query_cols)
    key_part_grad = jnp.einsum(
        "kgqs,qkgd->skd", score_grad, query_four, preferred_element_type=jnp.float32
    ).reshape(token_count, local_groups * HEAD_DIM)
    value_part_grad = jnp.einsum(
        "kgqs,qkgd->skd", prob_weights, grad_four, preferred_element_type=jnp.float32
    ).reshape(token_count, local_groups * HEAD_DIM)
    query_block_grad = rotate(query_rot_grad, row_positions, query_offset, -1.0).astype(
        jnp.bfloat16
    )

    def own_half(values):
        return lax.dynamic_slice_in_dim(values, parity * key_cols, key_cols, 1)

    def other_half(values):
        return lax.dynamic_slice_in_dim(values, (1 - parity) * key_cols, key_cols, 1)

    key_total, value_total = lax.psum((key_part_grad, value_part_grad), "width")
    if paired:
        sent_key, sent_value = from_partner(
            (other_half(key_total), other_half(value_total)), "ffn", 0
        )
        key_total = own_half(key_total) + sent_key
        value_total = own_half(value_total) + sent_value
    key_rows_gradient = rotate(key_total, positions, key_offset, -1.0).astype(jnp.bfloat16)
    value_rows_gradient = value_total.astype(jnp.bfloat16)
    query_rows_gradient = lax.all_gather(query_block_grad, "width", axis=0, tiled=True)
    input_part = (
        contract_last(query_rows_gradient, query_frozen_weight)
        + contract_last(key_rows_gradient, key_value_frozen_weight[0])
        + contract_last(value_rows_gradient, key_value_frozen_weight[1])
    )
    rank_grad_terms = jnp.concatenate(
        [
            contract_last(query_rows_gradient, query_up_map),
            contract_last(key_rows_gradient, key_value_up_maps[0]),
            contract_last(value_rows_gradient, key_value_up_maps[1]),
        ],
        axis=1,
    )
    rank_gradient = lax.psum(rank_grad_terms, "ffn").astype(jnp.bfloat16)
    input_sum = lax.psum_scatter(
        input_part.astype(jnp.bfloat16), "ffn", scatter_dimension=0, tiled=True
    ).astype(jnp.float32)
    own_rows = token_count // ffn_count
    rank_gradient_token_rows = lax.dynamic_slice_in_dim(
        rank_gradient, ffn_index * own_rows, own_rows, 0
    )
    hidden_gradient = (
        input_sum
        + adapter_scale
        * jnp.dot(rank_gradient_token_rows, down_flattened, preferred_element_type=jnp.float32)
    ).astype(jnp.bfloat16)
    down_map_gradient = (adapter_scale * contract_leading(rank_gradient, hidden_rows_full)).reshape(
        adapter_down.shape
    )
    query_up_map_gradient = adapter_scale * contract_leading(
        reduced_hidden[:, :ADAPTER_RANK], query_rows_gradient
    )
    key_value_up_maps_gradient = adapter_scale * jnp.stack(
        [
            contract_leading(reduced_hidden[:, ADAPTER_RANK : 2 * ADAPTER_RANK], key_rows_gradient),
            contract_leading(reduced_hidden[:, 2 * ADAPTER_RANK :], value_rows_gradient),
        ]
    )
    outer_terms = contract_last(attention_output, output_down_map)
    outer_rows = lax.psum(outer_terms, "ffn").astype(jnp.bfloat16)
    outer_product_rank = lax.all_gather(outer_rows, "width", axis=0, tiled=True)
    output_down_map_gradient = adapter_scale * lax.psum(
        contract_leading(output_token_rows, attention_output), "width"
    )
    output_up_map_gradient = adapter_scale * contract_leading(
        outer_product_rank, upstream_gradient_full
    )
    return (
        hidden_gradient,
        down_map_gradient,
        query_up_map_gradient,
        key_value_up_maps_gradient,
        output_down_map_gradient,
        output_up_map_gradient,
    )


def dot(left, right, dims=None):
    if dims is None:
        return jnp.dot(left, right, preferred_element_type=jnp.float32)
    return lax.dot_general(left, right, dims, preferred_element_type=jnp.float32)


def other_index(a, b):
    low = lax.rem(lax.rem(a, 2) + lax.rem(b, 2), 2)
    high = lax.rem(lax.div(a, 2) + lax.div(b, 2), 2)
    return 2 * high + low


def fused(
    score_scale,
    hidden_in, upstream_in, query_weight, key_value_weight, output_weight,
    cosine, sine, down, query_up, key_value_up, output_down, output_up,
    hidden_out, down_out, query_up_out, key_value_up_out, output_down_out, output_up_out,
    hid, up, wh, wg, buf, own, back, acc, land, tmp, key_state, value_state, key_grad, value_grad,
    low_own, low_sent, low_got, low, rank_sum, rank_pair, rank_got, outer, outer_pair, outer_got, misc,
    query_acc, key_value_acc,
    load_sem, weight_sem, grad_sem, gather_send, gather_recv, send_sem, recv_sem, back_send, back_recv,
    low_send, low_recv, misc_send, misc_recv, outer_send, outer_recv, land_send, land_recv,
    rank_send, rank_recv,
):
    bf16, f32 = jnp.bfloat16, jnp.float32
    rows, width = hidden_in.shape
    cols = CHUNK_HEADS * HEAD_DIM
    chunks = wh.shape[1] - 1
    side_cols = chunks * cols
    rank = ADAPTER_RANK
    pieces = 4 + 8 * chunks
    back_pieces = 4 * chunks + 4
    tiles = width // cols
    f = lax.axis_index("ffn")
    z = lax.axis_index("width")
    half = lax.div(z, 2)
    ahead = 1 - 2 * half
    inner = z + ahead
    outward = z - ahead
    is_end = (z == 0) | (z == 3)
    is_mid = (z == 1) | (z == 2)
    core_peer = f + 1 - 2 * lax.rem(f, 2)
    chip_peer = lax.rem(f + 2, 4)

    def copy(src, dst, send, recv, axis, target):
        return pltpu.make_async_remote_copy(
            src_ref=src, dst_ref=dst, send_sem=send, recv_sem=recv,
            device_id={axis: target}, device_id_type=MESH,
        )

    def side_of(side):
        return half + side * (1 - 2 * half)

    def loop(count, step, start=0):
        def run(i, carry):
            step(i)
            return carry
        lax.fori_loop(start, count, run, 0)

    load_hidden = pltpu.make_async_copy(hidden_in, hid.at[0], load_sem.at[0])
    load_upstream = pltpu.make_async_copy(upstream_in, up.at[0], load_sem.at[1])

    def load_weight(side, c):
        start = pl.multiple_of(side_of(side) * side_cols + c * cols, cols)
        return pltpu.make_async_copy(
            query_weight.at[:, pl.ds(start, cols)], wh.at[side, c], weight_sem.at[side, c]
        )

    def load_key_value(side, which):
        start = pl.multiple_of(side_of(side) * HEAD_DIM, HEAD_DIM)
        return pltpu.make_async_copy(
            key_value_weight.at[which, :, pl.ds(start, HEAD_DIM)],
            wh.at[side, chunks, :, pl.ds(which * HEAD_DIM, HEAD_DIM)],
            weight_sem.at[side, chunks + which],
        )

    def load_grad_weight(side, fetch):
        start = pl.multiple_of(side_of(side) * side_cols + lax.rem(fetch, chunks) * cols, cols)
        slot = lax.rem(fetch, 2)
        return pltpu.make_async_copy(
            output_weight.at[pl.ds(start, cols), :], wg.at[slot, side], grad_sem.at[slot, side]
        )

    load_hidden.start()
    for side in range(2):
        for which in range(2):
            load_key_value(side, which).start()
    for c in range(chunks):
        for side in range(2):
            load_weight(side, c).start()
    load_upstream.start()
    for fetch in range(2):
        for side in range(2):
            load_grad_weight(side, fetch).start()

    barrier = pltpu.get_barrier_semaphore()
    pl.semaphore_signal(barrier, inc=1, device_id={"ffn": core_peer}, device_id_type=MESH)
    pl.semaphore_signal(barrier, inc=1, device_id={"ffn": chip_peer}, device_id_type=MESH)
    pl.semaphore_signal(barrier, inc=1, device_id={"width": inner}, device_id_type=MESH)

    @pl.when(is_mid)
    def _():
        pl.semaphore_signal(barrier, inc=1, device_id={"width": outward}, device_id_type=MESH)
        pl.semaphore_wait(barrier, 4)

    @pl.when(is_end)
    def _():
        pl.semaphore_wait(barrier, 3)

    def gather(which, kind):
        source, full = ((hidden_in, hid), (upstream_in, up))[which]
        sems = gather_send.at[which, kind], gather_recv.at[which, kind]
        if kind == 0:
            return copy(source, full.at[1], *sems, "ffn", core_peer)
        if kind == 1:
            return copy(source, full.at[2], *sems, "ffn", chip_peer)
        return copy(full.at[2], full.at[3], *sems, "ffn", core_peer)

    for which in range(2):
        gather(which, 1).start()
        gather(which, 0).start()

    def send_away_end(s):
        return copy(buf.at[1, s], buf.at[1, s], send_sem.at[1, s], recv_sem.at[1, s], "width", inner)

    def send_away_mid(s):
        return copy(buf.at[1, s], buf.at[0, s], send_sem.at[1, s], recv_sem.at[0, s], "width", inner)

    def send_home(s):
        return copy(buf.at[0, s], buf.at[0, s], send_sem.at[0, s], recv_sem.at[0, s], "width", outward)

    def arrived(side, s):
        copy(
            buf.at[side, s], buf.at[side, s], send_sem.at[side, s], recv_sem.at[side, s], "width", inner
        ).wait_recv()

    def relay_home(s):
        arrived(0, s)
        buf[0, s] = (buf[0, s].astype(f32) + own[s].astype(f32)).astype(bf16)
        send_home(s).start()

    def push(s):
        @pl.when(is_end)
        def _():
            buf[1, s] = tmp[...].astype(bf16)
            send_away_end(s).start()

        @pl.when(is_mid)
        def _():
            arrived(1, s)
            buf[1, s] = (buf[1, s].astype(f32) + tmp[...]).astype(bf16)
            send_away_mid(s).start()

            @pl.when(s >= LAG)
            def _():
                relay_home(s - LAG)

    def hidden_step(s, c, j):
        tmp[...] = dot(hid[j], wh[1, c])
        own[s] = dot(hid[j], wh[0, c]).astype(bf16)
        push(s)

    def upstream_step(s, slot, j):
        tmp[...] = dot(up[j], wg[slot, 1], LAST)
        own[s] = dot(up[j], wg[slot, 0], LAST).astype(bf16)
        push(s)

    def wait_grad_weight(fetch):
        for side in range(2):
            load_grad_weight(side, fetch).wait()

    def next_grad_weight(fetch):
        for side in range(2):
            load_grad_weight(side, fetch).start()

    load_hidden.wait()
    for side in range(2):
        for which in range(2):
            load_key_value(side, which).wait()

    def near_hidden(i):
        @pl.when(i == 1)
        def _():
            gather(0, 0).wait_recv()

        @pl.when(i == 2)
        def _():
            for c in range(chunks):
                for side in range(2):
                    load_weight(side, c).wait()

        c = jnp.where(i < 2, chunks, lax.div(i, 2) - 1)
        hidden_step(i, c, lax.rem(i, 2))

    loop(2 + 2 * chunks, near_hidden)

    load_upstream.wait()
    gather(0, 1).wait_recv()
    gather(0, 2).start()
    gather(1, 0).wait_recv()

    def near_upstream(i):
        fetch = lax.div(i, 2)
        j = lax.rem(i, 2)

        @pl.when(j == 0)
        def _():
            wait_grad_weight(fetch)

        upstream_step(2 + 2 * chunks + i, lax.rem(fetch, 2), j)

        @pl.when(j == 1)
        def _():
            next_grad_weight(fetch + 2)

    loop(2 * chunks, near_upstream)

    gather(1, 1).wait_recv()
    gather(1, 2).start()
    gather(0, 2).wait_recv()
    gather(1, 2).wait_recv()

    def low_copy(slot, target_slot, target):
        return copy(
            low_sent.at[slot], low_got.at[target_slot], low_send.at[slot], low_recv.at[target_slot],
            "width", target,
        )

    def low_terms(j):
        low_own[j, : 3 * rank] = dot(down[...], hid[j], LAST)
        low_own[j, 3 * rank :] = dot(output_up[...], up[j], LAST)
        acc[j] = jnp.zeros(acc.shape[1:], f32)

    loop(4, low_terms)
    rank_sum[...] = jnp.zeros_like(rank_sum)
    query_acc[...] = jnp.zeros_like(query_acc)
    key_value_acc[...] = jnp.zeros_like(key_value_acc)

    @pl.when(is_end)
    def _():
        low_sent[0] = low_own[...].astype(bf16)
        low_copy(0, 1, inner).start()

    @pl.when(is_mid)
    def _():
        low_copy(0, 1, inner).wait_recv()
        low_own[...] += low_got[1].astype(f32)
        low_sent[0] = low_own[...].astype(bf16)
        low_copy(0, 0, inner).start()

    def far_steps(i):
        c = jnp.where(i < 2, chunks, lax.div(i, 2) - 1)
        j = 2 + lax.rem(i, 2)
        first = 2 + 4 * chunks
        s = first + jnp.where(i < 2, i, 2 * i - 2)

        @pl.when((i == 4) & is_mid)
        def _():
            low_copy(1, 0, outward).wait_recv()
            got = low_got[0].astype(f32)
            low_sent[1] = (low_own[...] - low_got[1].astype(f32) + got).astype(bf16)
            low_copy(1, 0, outward).start()
            low[...] = (low_own[...] + got).astype(bf16)

        hidden_step(s, c, j)

        @pl.when(i >= 2)
        def _():
            fetch = chunks + c

            @pl.when(j == 2)
            def _():
                wait_grad_weight(fetch)

            upstream_step(s + 1, lax.rem(fetch, 2), j)

            @pl.when((j == 3) & (fetch + 2 < 2 * chunks))
            def _():
                next_grad_weight(fetch + 2)

    loop(2 + 2 * chunks, far_steps)

    @pl.when(is_mid)
    def _():
        loop(pieces, relay_home, pieces - LAG)

    def piece_of(kind, c, j):
        near = (0, 2, 2 + 2 * chunks)[kind] + 2 * c + j
        first = 2 + 4 * chunks
        far = first + j - 2 if kind == 0 else first + kind + 1 + 4 * c + 2 * (j - 2)
        return near if j < 2 else far

    even = lax.broadcasted_iota(jnp.int32, (rows, HEAD_DIM), 1) % 2 == 0

    def turned(values, start, direction):
        following = pltpu.roll(values, HEAD_DIM - 1, 1)
        preceding = pltpu.roll(values, 1, 1)
        partner = jnp.where(even, -following, preceding)
        at = pl.ds(start, rows)
        return values * cosine[at, :] + direction * partner * sine[at, :]

    def back_home(p):
        return copy(back.at[0, p], back.at[0, p], back_send.at[0, p], back_recv.at[0, p], "width", inner)

    def back_across(p):
        return copy(back.at[0, p], back.at[1, p], back_send.at[0, p], back_recv.at[1, p], "width", inner)

    def back_out(p):
        return copy(back.at[1, p], back.at[1, p], back_send.at[1, p], back_recv.at[1, p], "width", outward)

    def misc_copy(slot, target_slot, target):
        return copy(
            misc.at[slot], misc.at[target_slot], misc_send.at[slot], misc_recv.at[target_slot],
            "width", target,
        )

    outer_core = copy(outer, outer_got.at[0], outer_send.at[0], outer_recv.at[0], "ffn", core_peer)
    outer_chip = copy(outer_pair, outer_got.at[1], outer_send.at[1], outer_recv.at[1], "ffn", chip_peer)

    @pl.when(is_end)
    def _():
        low_copy(0, 0, inner).wait_recv()
        low[...] = (low_own[...] + low_got[0].astype(f32)).astype(bf16)
        outer[...] = jnp.zeros_like(outer)
        key_grad[...] = jnp.zeros_like(key_grad)
        value_grad[...] = jnp.zeros_like(value_grad)
        head_col = pl.multiple_of(half * HEAD_DIM, HEAD_DIM)
        key_map = key_value_up[0, :, pl.ds(head_col, HEAD_DIM)]
        value_map = key_value_up[1, :, pl.ds(head_col, HEAD_DIM)]
        for j in range(4):
            s = piece_of(0, 0, j)
            arrived(0, s)
            start = pl.multiple_of(other_index(f, j) * rows, rows)
            total = buf[0, s].astype(f32) + own[s].astype(f32)
            key_sum = total[:, :HEAD_DIM] + adapter_scale * dot(low[j, rank : 2 * rank], key_map, FIRST)
            value_sum = total[:, HEAD_DIM:] + adapter_scale * dot(
                low[j, 2 * rank : 3 * rank], value_map, FIRST
            )
            key_state[pl.ds(start, rows), :] = turned(key_sum, start, 1.0).astype(bf16)
            value_state[pl.ds(start, rows), :] = value_sum.astype(bf16)

        def heads(c):
            for j in range(4):
                for kind in (1, 2):
                    arrived(0, piece_of(kind, c, j))

            def one_head(head):
                lane = pl.multiple_of(head * HEAD_DIM, HEAD_DIM)
                lanes = pl.ds(lane, HEAD_DIM)
                first = pl.multiple_of(half * side_cols + c * cols + lane, HEAD_DIM)
                query_map = query_up[:, pl.ds(first, HEAD_DIM)]
                grad_map = output_down[:, pl.ds(first, HEAD_DIM)]
                map_grad = jnp.zeros((rank, HEAD_DIM), f32)
                for block in range(BLOCKS):
                    start, stop = block * rows, (block + 1) * rows
                    j = other_index(f, block)
                    near = j < 2
                    base = 2 + 4 * chunks
                    s_q = jnp.where(near, 2 + 2 * c + j, base + 2 + 4 * c + 2 * (j - 2))
                    s_g = jnp.where(near, 2 + 2 * chunks + 2 * c + j, base + 3 + 4 * c + 2 * (j - 2))
                    query_sum = buf[0, s_q, :, lanes].astype(f32) + own[s_q, :, lanes].astype(f32)
                    query_sum += adapter_scale * dot(low[j, :rank], query_map, FIRST)
                    query = turned(query_sum, start, 1.0).astype(bf16)
                    grad_sum = buf[0, s_g, :, lanes].astype(f32) + own[s_g, :, lanes].astype(f32)
                    out_rank = low[j, 3 * rank :]
                    grad = (grad_sum + adapter_scale * dot(out_rank, grad_map, FIRST)).astype(bf16)
                    key_part = key_state[:stop, :]
                    value_part = value_state[:stop, :]
                    scores = dot(query, key_part, LAST) * score_scale
                    row = start + lax.broadcasted_iota(jnp.int32, (rows, stop), 0)
                    column = lax.broadcasted_iota(jnp.int32, (rows, stop), 1)
                    scores = jnp.where(row >= column, scores, -jnp.inf)
                    shifted = jnp.exp(scores - jnp.max(scores, axis=1, keepdims=True))
                    probs = shifted * (1.0 / jnp.sum(shifted, axis=1, keepdims=True))
                    weights = probs.astype(bf16)
                    attended = dot(weights, value_part).astype(bf16)
                    outer[j] += dot(grad_map, attended, LAST)
                    map_grad += dot(out_rank, attended)
                    prob_grad = dot(grad, value_part, LAST)
                    delta = jnp.sum(
                        grad.astype(f32) * attended.astype(f32), axis=1, keepdims=True
                    )
                    score_grad = (probs * ((prob_grad - delta) * score_scale)).astype(bf16)
                    p = 4 * c + lax.rem(j + 2, 4)
                    back[0, p, :, lanes] = turned(dot(score_grad, key_part), start, -1.0).astype(bf16)
                    key_grad[:stop, :] += dot(score_grad, query, FIRST)
                    value_grad[:stop, :] += dot(weights, grad, FIRST)
                misc[0, 4 + c, :, lanes] = adapter_scale * map_grad

            loop(CHUNK_HEADS, one_head)
            for k in range(4):
                back_home(4 * c + k).start()

        loop(chunks, heads)
        outer_core.start()
        outer_core.wait_recv()
        for j in range(4):
            outer_pair[j] = outer[j] + outer_got[0, j + 1 - 2 * (j % 2)]
        outer_chip.start()
        for k in range(4):
            j = (k + 2) % 4
            start = pl.multiple_of(other_index(f, j) * rows, rows)
            key_block = turned(key_grad[pl.ds(start, rows), :], start, -1.0)
            back[0, 4 * chunks + k, :, :HEAD_DIM] = key_block.astype(bf16)
            back[0, 4 * chunks + k, :, HEAD_DIM:] = value_grad[pl.ds(start, rows), :].astype(bf16)
            back_home(4 * chunks + k).start()
        outer_chip.wait_recv()
        for j in range(4):
            misc[0, j] = outer_pair[j] + outer_got[1, (j + 2) % 4]
        misc_copy(0, 0, inner).start()

    def back_arrived(side, p):
        copy(
            back.at[side, p], back.at[side, p], back_send.at[side, p], back_recv.at[side, p],
            "width", inner,
        ).wait_recv()

    def absorb(side, p):
        c = lax.div(p, 4)
        j = lax.rem(lax.rem(p, 4) + 2, 4)
        step = min(2 * cols, width)
        for n in range(width // step):
            at = slice(n * step, (n + 1) * step)
            acc[j, :, at] += dot(back[side, p], wh[side, c, at, :], LAST)
        which = side_of(side)

        @pl.when(c < chunks)
        def _():
            column = pl.multiple_of(which * side_cols + c * cols, cols)
            rank_sum[j, :rank] += dot(query_up[:, pl.ds(column, cols)], back[side, p], LAST)
            query_acc[which * chunks + c] += dot(low[j, :rank], back[side, p])

        @pl.when(c == chunks)
        def _():
            column = pl.multiple_of(which * HEAD_DIM, HEAD_DIM)
            for i in range(2):
                values = back[side, p, :, i * HEAD_DIM : (i + 1) * HEAD_DIM]
                at = slice((i + 1) * rank, (i + 2) * rank)
                rank_sum[j, at] += dot(key_value_up[i, :, pl.ds(column, HEAD_DIM)], values, LAST)
                key_value_acc[which, i] += dot(low[j, at], values)

    def back_step(t):
        @pl.when((t < back_pieces) & is_mid)
        def _():
            back_arrived(0, t)
            back_across(t).start()

        @pl.when(t >= BACK_LAG)
        def _():
            back_arrived(1, t - BACK_LAG)

            @pl.when(is_mid)
            def _():
                back_out(t - BACK_LAG).start()

        def absorb_side(side):
            p = t - BACK_LAG * side

            @pl.when((p >= 0) & (p < back_pieces))
            def _():
                absorb(side, p)

        loop(2, absorb_side)

    def land_copy(first, count, slot, at, sem, axis, target):
        return copy(
            own.at[pl.ds(first, count)], land.at[slot, pl.ds(at, count)],
            land_send.at[sem], land_recv.at[sem], axis, target,
        )

    far_pair = land_copy(0, tiles, 1, 0, 0, "ffn", core_peer)
    near_pair = land_copy(tiles, tiles, 0, 0, 1, "ffn", core_peer)
    parts = 4
    per_part = tiles // parts
    chip_parts = [
        land_copy(2 * tiles + n * per_part, per_part, 2, n * per_part, 2 + n, "ffn", chip_peer)
        for n in range(parts)
    ]

    @pl.when(is_mid)
    def _():
        loop(pieces, lambda s: send_home(s).wait_send())

    loop(back_pieces - 2 + BACK_LAG, back_step)
    for n in range(tiles):
        own[n] = acc[3, :, n * cols : (n + 1) * cols].astype(bf16)
    far_pair.start()
    loop(back_pieces + BACK_LAG, back_step, back_pieces - 2 + BACK_LAG)
    far_pair.wait_recv()
    for n in range(tiles):
        pair = acc[2, :, n * cols : (n + 1) * cols] + land[1, n].astype(f32)
        own[2 * tiles + n] = pair.astype(bf16)
    for part in chip_parts[: parts // 2]:
        part.start()
    rank_core = copy(rank_sum, rank_got.at[0], rank_send.at[0], rank_recv.at[0], "ffn", core_peer)
    rank_chip = copy(rank_pair, rank_got.at[1], rank_send.at[1], rank_recv.at[1], "ffn", chip_peer)
    rank_core.start()
    for n in range(tiles):
        own[tiles + n] = acc[1, :, n * cols : (n + 1) * cols].astype(bf16)
    near_pair.start()
    rank_core.wait_recv()
    for j in range(4):
        rank_pair[j] = rank_sum[j] + rank_got[0, j + 1 - 2 * (j % 2)]
    rank_chip.start()
    for part in chip_parts[parts // 2 :]:
        part.start()

    @pl.when(is_mid)
    def _():
        misc_copy(0, 0, inner).wait_recv()
        misc_copy(0, 1, inner).start()
        misc_copy(1, 1, outward).wait_recv()
        misc_copy(1, 1, outward).start()

    @pl.when(is_end)
    def _():
        misc_copy(1, 1, inner).wait_recv()

    outer_rank = [(misc[0, j] + misc[1, j]).astype(bf16) for j in range(4)]
    for side in range(2):
        for c in range(chunks):
            column = pl.multiple_of(side_of(side) * side_cols + c * cols, cols)
            output_down_out[:, pl.ds(column, cols)] = misc[side, 4 + c]
    for c in range(2 * chunks):
        query_up_out[:, c * cols : (c + 1) * cols] = adapter_scale * query_acc[c]
    for which in range(2):
        for i in range(2):
            at = slice(which * HEAD_DIM, (which + 1) * HEAD_DIM)
            key_value_up_out[i, :, at] = adapter_scale * key_value_acc[which, i]
    total = dot(outer_rank[0], up[0])
    for j in range(1, 4):
        total += dot(outer_rank[j], up[j])
    output_up_out[...] = adapter_scale * total
    rank_chip.wait_recv()
    ranks = [(rank_pair[j] + rank_got[1, (j + 2) % 4]).astype(bf16) for j in range(4)]
    total = dot(ranks[0], hid[0])
    for j in range(1, 4):
        total += dot(ranks[j], hid[j])
    down_out[...] = adapter_scale * total
    near_pair.wait_recv()
    for n in range(tiles):
        at = slice(n * cols, (n + 1) * cols)
        acc[0, :, at] += land[0, n].astype(f32) + adapter_scale * dot(ranks[0], down[:, at], FIRST)
    for part_index, part in enumerate(chip_parts):
        part.wait_recv()
        for n in range(part_index * per_part, (part_index + 1) * per_part):
            at = slice(n * cols, (n + 1) * cols)
            hidden_out[:, at] = (acc[0, :, at] + land[2, n].astype(f32)).astype(bf16)

    for which in range(2):
        for kind in range(3):
            gather(which, kind).wait_send()
    loop(pieces, lambda s: send_away_end(s).wait_send())
    loop(back_pieces, lambda p: back_home(p).wait_send())
    low_copy(0, 0, inner).wait_send()
    misc_copy(0, 0, inner).wait_send()

    @pl.when(is_mid)
    def _():
        loop(back_pieces, lambda p: back_out(p).wait_send())
        low_copy(1, 0, outward).wait_send()
        misc_copy(1, 1, outward).wait_send()

    @pl.when(is_end)
    def _():
        outer_core.wait_send()
        outer_chip.wait_send()

    far_pair.wait_send()
    near_pair.wait_send()
    for part in chip_parts:
        part.wait_send()
    rank_core.wait_send()
    rank_chip.wait_send()


def one_kernel(
    hidden,
    upstream,
    query_frozen_weight,
    key_value_frozen_weight,
    output_frozen_weight,
    adapter_down,
    query_up_map,
    key_value_up_maps,
    output_down_map,
    output_up,
):
    bf16, f32 = jnp.bfloat16, jnp.float32
    rows, width = hidden.shape
    query_cols = query_frozen_weight.shape[1]
    cols = CHUNK_HEADS * HEAD_DIM
    chunks = query_cols // 2 // cols
    pieces = 4 + 8 * chunks
    back_pieces = 4 * chunks + 4
    tiles = width // cols
    tokens = 4 * rows
    rank = ADAPTER_RANK
    head_dims = np.arange(HEAD_DIM)
    frequency = np.exp((head_dims - head_dims % 2) * (-math.log(rope_base) / HEAD_DIM))
    angles = np.arange(tokens)[:, None] * frequency[None, :]
    cosine = jnp.asarray(np.cos(angles), f32)
    sine = jnp.asarray(np.sin(angles), f32)
    vmem = pl.BlockSpec(memory_space=pltpu.VMEM)
    hbm = pl.BlockSpec(memory_space=pl.ANY)
    dma = pltpu.SemaphoreType.DMA
    shape = jax.ShapeDtypeStruct
    outputs = pl.pallas_call(
        functools.partial(fused, 1.0 / math.sqrt(HEAD_DIM)),
        out_shape=(
            shape((rows, width), bf16),
            shape((3 * rank, width), f32),
            shape(query_up_map.shape, f32),
            shape(key_value_up_maps.shape, f32),
            shape(output_down_map.shape, f32),
            shape(output_up.shape, f32),
        ),
        in_specs=[hbm] * 5 + [vmem] * 7,
        out_specs=(vmem,) * 6,
        scratch_shapes=[
            pltpu.VMEM((4, rows, width), bf16),
            pltpu.VMEM((4, rows, width), bf16),
            pltpu.VMEM((2, chunks + 1, width, cols), bf16),
            pltpu.VMEM((2, 2, cols, width), bf16),
            pltpu.VMEM((2, pieces, rows, cols), bf16),
            pltpu.VMEM((pieces, rows, cols), bf16),
            pltpu.VMEM((2, back_pieces, rows, cols), bf16),
            pltpu.VMEM((4, rows, width), f32),
            pltpu.VMEM((3, tiles, rows, cols), bf16),
            pltpu.VMEM((rows, cols), f32),
            pltpu.VMEM((tokens, HEAD_DIM), bf16),
            pltpu.VMEM((tokens, HEAD_DIM), bf16),
            pltpu.VMEM((tokens, HEAD_DIM), f32),
            pltpu.VMEM((tokens, HEAD_DIM), f32),
            pltpu.VMEM((4, 4 * rank, rows), f32),
            pltpu.VMEM((2, 4, 4 * rank, rows), bf16),
            pltpu.VMEM((2, 4, 4 * rank, rows), bf16),
            pltpu.VMEM((4, 4 * rank, rows), bf16),
            pltpu.VMEM((4, 3 * rank, rows), f32),
            pltpu.VMEM((4, 3 * rank, rows), f32),
            pltpu.VMEM((2, 4, 3 * rank, rows), f32),
            pltpu.VMEM((4, rank, rows), f32),
            pltpu.VMEM((4, rank, rows), f32),
            pltpu.VMEM((2, 4, rank, rows), f32),
            pltpu.VMEM((2, 4 + chunks, rank, cols), f32),
            pltpu.VMEM((2 * chunks, rank, cols), f32),
            pltpu.VMEM((2, 2, rank, HEAD_DIM), f32),
            dma((2,)),
            dma((2, chunks + 2)),
            dma((2, 2)),
            dma((2, 3)),
            dma((2, 3)),
            dma((2, pieces)),
            dma((2, pieces)),
            dma((2, back_pieces)),
            dma((2, back_pieces)),
            dma((2,)),
            dma((2,)),
            dma((2,)),
            dma((2,)),
            dma((2,)),
            dma((2,)),
            dma((6,)),
            dma((6,)),
            dma((2,)),
            dma((2,)),
        ],
        compiler_params=pltpu.CompilerParams(
            collective_id=0, has_side_effects=True, vmem_limit_bytes=67_000_000
        ),
    )(
        hidden,
        upstream,
        query_frozen_weight,
        key_value_frozen_weight,
        output_frozen_weight,
        cosine,
        sine,
        adapter_down.reshape(3 * rank, width),
        query_up_map,
        key_value_up_maps,
        output_down_map,
        output_up,
    )
    return (outputs[0], outputs[1].reshape(adapter_down.shape), *outputs[2:])


def by_shape(*arrays):
    rows, width = arrays[0].shape
    cols = CHUNK_HEADS * HEAD_DIM
    fits = (
        arrays[3].shape[2] == 2 * HEAD_DIM
        and lax.axis_size("width") == 4
        and lax.axis_size("ffn") == 4
        and arrays[2].shape[1] % (2 * cols) == 0
        and rows == cols
        and width % (4 * cols) == 0
    )
    return one_kernel(*arrays) if fits else shards(*arrays)


def solution(mesh):
    placed = (
        P(("groups", "ffn"), "width"),
        P(("groups", "ffn"), "width"),
        P("width", "ffn"),
        P(None, "width", "ffn"),
        P("ffn", "width"),
        P("groups", None, "width"),
        P("groups", "ffn"),
        P("groups", None, "ffn"),
        P("groups", "ffn"),
        P("groups", "width"),
    )
    return jax.shard_map(
        by_shape,
        mesh=mesh,
        in_specs=placed,
        out_specs=(
            P(("groups", "ffn"), "width"),
            P("groups", None, "width"),
            P("groups", "ffn"),
            P("groups", None, "ffn"),
            P("groups", "ffn"),
            P("groups", "width"),
        ),
        check_vma=False,
    )
```

time: 518 us -> 239 us (0.46)
  the two profiles are of different devices: /device:TPU:8 before, /device:TPU:0 now
where the time goes in v1:
time: 239 us; the launch traced here: 238 us
  Pallas kernels  228 us (95%)
  local copies, waits for them, and re-layouts  10.1 us (4%)
    pallas_call x1, Pallas kernels, one_kernel(): pl.pallas_call(functools.partial(fused, 1.0 / math.sqrt(HEAD_DIM)), out_s...  228 us
    unnamed x6, local copies, waits for them, and re-layouts  10.1 us

profile of v1, /device:TPU:0, one launch (start us, length us, event | category | flops | bytes accessed | tf_op | source)
XLA Modules:
  0.0 238.4 jit_solution(2587902571130305069)
XLA Ops:
  0.6 227.7 %shard_map.163 = (bf16[256,2048]{1,0:T(8,128)(2,1)}, f32[48,2048]{1,0:T(8,128)}, f32[16,2048]{1,0:T(8,128)}, f32[2,16,256]{2,1,0:T(8,128)}, f32[16,2048]{1,0:T(8,128)}, /*index=5*/f32[16,2048]{1,0:T(8,128)}) custom-call(bf16[256,2048]{1,0:T(8,128)(2,1)} %hidden_in.1, bf16[256,2048]{1,0:T(8,128)(2,1)} %upstream_in.1, bf16[2048,2048]{1,0:T(8,128)(2,1)} %query_weight.1, ...), custom_call_target="tpu_custom_call" | custom-call | tf_op jit(solution)/shard_map/pallas_call | solution.py:874
  228.3 2.3 copy.24
  230.6 1.8 copy.25
  232.4 1.6 copy.26
  233.9 1.4 copy.27
  235.3 1.6 copy.28
  236.9 1.6 copy.29

commit v2 on v1

--- a/solution.py
+++ b/solution.py
@@ -15,7 +15,6 @@
 CHUNK_HEADS = 2
 BLOCKS = 4
 LAG = 3
-BACK_LAG = 2
 MESH = pl.DeviceIdType.MESH
 LAST = (((1,), (1,)), ((), ()))
 FIRST = (((0,), (0,)), ((), ()))
@@ -279,23 +278,31 @@
 def fused(
     score_scale,
     hidden_in, upstream_in, query_weight, key_value_weight, output_weight,
-    cosine, sine, down, query_up, key_value_up, output_down, output_up,
-    hidden_out, down_out, query_up_out, key_value_up_out, output_down_out, output_up_out,
-    hid, up, wh, wg, buf, own, back, acc, land, tmp, key_state, value_state, key_grad, value_grad,
-    low_own, low_sent, low_got, low, rank_sum, rank_pair, rank_got, outer, outer_pair, outer_got, misc,
-    query_acc, key_value_acc,
-    load_sem, weight_sem, grad_sem, gather_send, gather_recv, send_sem, recv_sem, back_send, back_recv,
-    low_send, low_recv, misc_send, misc_recv, outer_send, outer_recv, land_send, land_recv,
-    rank_send, rank_recv,
+    *refs,
 ):
+    small_in, results, small, staged = refs[:7], refs[7:13], refs[13:20], refs[20:26]
+    (
+        hid, up, wh, wg, buf, own, back, acc, land, tmp, key_state, value_state, key_grad, value_grad,
+        low_own, low_sent, low_got, low, rank_sum, rank_pair, rank_got, rank_far, outer, outer_pair,
+        outer_got, misc, query_acc, key_value_acc,
+        load_sem, weight_sem, grad_sem, gather_send, gather_recv, send_sem, recv_sem, back_send,
+        back_recv, low_send, low_recv, misc_send, misc_recv, outer_send, outer_recv, land_send,
+        land_recv, rank_send, rank_recv, small_sem, result_sem,
+    ) = refs[26:]
+    cosine, sine, down, query_up, key_value_up, output_down, output_up = small
+    hidden_out, down_out, query_up_out, key_value_up_out, output_down_out, output_up_out = staged
     bf16, f32 = jnp.bfloat16, jnp.float32
     rows, width = hidden_in.shape
     cols = CHUNK_HEADS * HEAD_DIM
     chunks = wh.shape[1] - 1
     side_cols = chunks * cols
     rank = ADAPTER_RANK
-    pieces = 4 + 8 * chunks
-    back_pieces = 4 * chunks + 4
+    last = chunks - 1
+    near_end = 2 + 4 * last
+    far_end = 2 * near_end
+    pieces = far_end + 8
+    far_back = 4 + 2 * chunks
+    back_pieces = 4 + 4 * chunks
     tiles = width // cols
     f = lax.axis_index("ffn")
     z = lax.axis_index("width")
@@ -341,32 +348,33 @@
         )
 
     def load_grad_weight(side, fetch):
-        start = pl.multiple_of(side_of(side) * side_cols + lax.rem(fetch, chunks) * cols, cols)
+        c = jnp.where(fetch == 2 * last, last, lax.rem(fetch, last))
+        start = pl.multiple_of(side_of(side) * side_cols + c * cols, cols)
         slot = lax.rem(fetch, 2)
         return pltpu.make_async_copy(
             output_weight.at[pl.ds(start, cols), :], wg.at[slot, side], grad_sem.at[slot, side]
         )
 
+    load_small = [
+        pltpu.make_async_copy(source, target, small_sem.at[n])
+        for n, (source, target) in enumerate(zip(small_in, small))
+    ]
+    barrier = pltpu.get_barrier_semaphore()
+    pl.semaphore_signal(barrier, inc=1, device_id={"ffn": core_peer}, device_id_type=MESH)
+    pl.semaphore_signal(barrier, inc=1, device_id={"ffn": chip_peer}, device_id_type=MESH)
+    pl.semaphore_signal(barrier, inc=1, device_id={"width": inner}, device_id_type=MESH)
+
+    @pl.when(is_mid)
+    def _():
+        pl.semaphore_signal(barrier, inc=1, device_id={"width": outward}, device_id_type=MESH)
+
     load_hidden.start()
     for side in range(2):
         for which in range(2):
             load_key_value(side, which).start()
-    for c in range(chunks):
-        for side in range(2):
-            load_weight(side, c).start()
-    load_upstream.start()
-    for fetch in range(2):
-        for side in range(2):
-            load_grad_weight(side, fetch).start()
-
-    barrier = pltpu.get_barrier_semaphore()
-    pl.semaphore_signal(barrier, inc=1, device_id={"ffn": core_peer}, device_id_type=MESH)
-    pl.semaphore_signal(barrier, inc=1, device_id={"ffn": chip_peer}, device_id_type=MESH)
-    pl.semaphore_signal(barrier, inc=1, device_id={"width": inner}, device_id_type=MESH)
 
     @pl.when(is_mid)
     def _():
-        pl.semaphore_signal(barrier, inc=1, device_id={"width": outward}, device_id_type=MESH)
         pl.semaphore_wait(barrier, 4)
 
     @pl.when(is_end)
@@ -385,6 +393,15 @@
     for which in range(2):
         gather(which, 1).start()
         gather(which, 0).start()
+    for c in range(chunks):
+        for side in range(2):
+            load_weight(side, c).start()
+    load_upstream.start()
+    for fetch in range(2):
+        for side in range(2):
+            load_grad_weight(side, fetch).start()
+    for load in load_small:
+        load.start()
 
     def send_away_end(s):
         return copy(buf.at[1, s], buf.at[1, s], send_sem.at[1, s], recv_sem.at[1, s], "width", inner)
@@ -443,48 +460,6 @@
     for side in range(2):
         for which in range(2):
             load_key_value(side, which).wait()
-
-    def near_hidden(i):
-        @pl.when(i == 1)
-        def _():
-            gather(0, 0).wait_recv()
-
-        @pl.when(i == 2)
-        def _():
-            for c in range(chunks):
-                for side in range(2):
-                    load_weight(side, c).wait()
-
-        c = jnp.where(i < 2, chunks, lax.div(i, 2) - 1)
-        hidden_step(i, c, lax.rem(i, 2))
-
-    loop(2 + 2 * chunks, near_hidden)
-
-    load_upstream.wait()
-    gather(0, 1).wait_recv()
-    gather(0, 2).start()
-    gather(1, 0).wait_recv()
-
-    def near_upstream(i):
-        fetch = lax.div(i, 2)
-        j = lax.rem(i, 2)
-
-        @pl.when(j == 0)
-        def _():
-            wait_grad_weight(fetch)
-
-        upstream_step(2 + 2 * chunks + i, lax.rem(fetch, 2), j)
-
-        @pl.when(j == 1)
-        def _():
-            next_grad_weight(fetch + 2)
-
-    loop(2 * chunks, near_upstream)
-
-    gather(1, 1).wait_recv()
-    gather(1, 2).start()
-    gather(0, 2).wait_recv()
-    gather(1, 2).wait_recv()
 
     def low_copy(slot, target_slot, target):
         return copy(
@@ -495,66 +470,130 @@
     def low_terms(j):
         low_own[j, : 3 * rank] = dot(down[...], hid[j], LAST)
         low_own[j, 3 * rank :] = dot(output_up[...], up[j], LAST)
-        acc[j] = jnp.zeros(acc.shape[1:], f32)
-
-    loop(4, low_terms)
+
+    def forward_step(s):
+        late = s >= near_end
+        r = s - jnp.where(late, near_end, 0) - 2
+        key_value = r < 0
+        full = jnp.maximum(r, 0)
+        tail = s - far_end
+        in_last = tail >= 0
+        tail = jnp.maximum(tail, 0)
+        quarter = lax.rem(full, 4)
+        c = jnp.where(key_value, chunks, jnp.where(in_last, last, lax.div(full, 4)))
+        grad = jnp.where(in_last, lax.rem(tail, 2), lax.div(quarter, 2))
+        is_grad = (grad == 1) & (r >= 0)
+        j = jnp.where(key_value, r + 2, lax.rem(quarter, 2)) + jnp.where(late, 2, 0)
+        j = jnp.where(in_last, lax.rem(lax.div(tail, 2) + 2, 4), j)
+        fetch = jnp.where(in_last, 2 * last, c + jnp.where(late, last, 0))
+
+        @pl.when(s == 1)
+        def _():
+            gather(0, 0).wait_recv()
+
+        @pl.when(s == 2)
+        def _():
+            for n in range(chunks):
+                for side in range(2):
+                    load_weight(side, n).wait()
+
+        @pl.when(s == 4)
+        def _():
+            load_upstream.wait()
+
+        @pl.when(s == 5)
+        def _():
+            gather(1, 0).wait_recv()
+
+        @pl.when(s == 8)
+        def _():
+            for load in load_small:
+                load.wait()
+
+        @pl.when(s == near_end)
+        def _():
+            gather(0, 1).wait_recv()
+            gather(0, 2).start()
+
+        @pl.when(s == near_end + 1)
+        def _():
+            gather(0, 2).wait_recv()
+
+        @pl.when(s == near_end + 4)
+        def _():
+            gather(1, 1).wait_recv()
+            gather(1, 2).start()
+
+        @pl.when(s == near_end + 5)
+        def _():
+            gather(1, 2).wait_recv()
+
+        near_low = (s == 8) | (s == 9)
+        far_low = (s == near_end + 4) | (s == near_end + 5)
+
+        @pl.when(near_low | far_low)
+        def _():
+            low_terms(jnp.where(s < near_end, s - 8, s - near_end - 2))
+
+        @pl.when((s >= 10) & (s < 14))
+        def _():
+            acc[s - 10] = jnp.zeros(acc.shape[1:], f32)
+
+        @pl.when((s == near_end + 6) & is_end)
+        def _():
+            low_sent[0] = low_own[...].astype(bf16)
+            low_copy(0, 1, inner).start()
+
+        @pl.when((s == near_end + 6) & is_mid)
+        def _():
+            low_copy(0, 1, inner).wait_recv()
+            low_sent[0] = (low_own[...] + low_got[1].astype(f32)).astype(bf16)
+            low_copy(0, 0, inner).start()
+
+        @pl.when((s == near_end + 6 + LAG) & is_mid)
+        def _():
+            low_copy(1, 0, outward).wait_recv()
+            total = low_own[...] + low_got[0].astype(f32)
+            low_sent[1] = total.astype(bf16)
+            low_copy(1, 0, outward).start()
+            low[...] = (total + low_got[1].astype(f32)).astype(bf16)
+
+        @pl.when(~is_grad)
+        def _():
+            hidden_step(s, c, j)
+
+        @pl.when(is_grad)
+        def _():
+            first = jnp.where(in_last, s == far_end + 1, lax.rem(j, 2) == 0)
+
+            @pl.when(first)
+            def _():
+                wait_grad_weight(fetch)
+
+            upstream_step(s, lax.rem(fetch, 2), j)
+
+            @pl.when((lax.rem(j, 2) == 1) & (fetch + 2 <= 2 * last) & (s < far_end))
+            def _():
+                next_grad_weight(fetch + 2)
+
     rank_sum[...] = jnp.zeros_like(rank_sum)
     query_acc[...] = jnp.zeros_like(query_acc)
     key_value_acc[...] = jnp.zeros_like(key_value_acc)
-
-    @pl.when(is_end)
-    def _():
-        low_sent[0] = low_own[...].astype(bf16)
-        low_copy(0, 1, inner).start()
-
-    @pl.when(is_mid)
-    def _():
-        low_copy(0, 1, inner).wait_recv()
-        low_own[...] += low_got[1].astype(f32)
-        low_sent[0] = low_own[...].astype(bf16)
-        low_copy(0, 0, inner).start()
-
-    def far_steps(i):
-        c = jnp.where(i < 2, chunks, lax.div(i, 2) - 1)
-        j = 2 + lax.rem(i, 2)
-        first = 2 + 4 * chunks
-        s = first + jnp.where(i < 2, i, 2 * i - 2)
-
-        @pl.when((i == 4) & is_mid)
-        def _():
-            low_copy(1, 0, outward).wait_recv()
-            got = low_got[0].astype(f32)
-            low_sent[1] = (low_own[...] - low_got[1].astype(f32) + got).astype(bf16)
-            low_copy(1, 0, outward).start()
-            low[...] = (low_own[...] + got).astype(bf16)
-
-        hidden_step(s, c, j)
-
-        @pl.when(i >= 2)
-        def _():
-            fetch = chunks + c
-
-            @pl.when(j == 2)
-            def _():
-                wait_grad_weight(fetch)
-
-            upstream_step(s + 1, lax.rem(fetch, 2), j)
-
-            @pl.when((j == 3) & (fetch + 2 < 2 * chunks))
-            def _():
-                next_grad_weight(fetch + 2)
-
-    loop(2 + 2 * chunks, far_steps)
-
-    @pl.when(is_mid)
-    def _():
-        loop(pieces, relay_home, pieces - LAG)
+    loop(pieces, forward_step)
 
     def piece_of(kind, c, j):
-        near = (0, 2, 2 + 2 * chunks)[kind] + 2 * c + j
-        first = 2 + 4 * chunks
-        far = first + j - 2 if kind == 0 else first + kind + 1 + 4 * c + 2 * (j - 2)
-        return near if j < 2 else far
+        if kind == 0:
+            return j if j < 2 else near_end + j - 2
+        spread = jnp.where(j < 2, 2 + j, near_end + j) + 4 * c + 2 * (kind - 1)
+        return jnp.where(c == last, far_end + 2 * lax.rem(j + 2, 4) + kind - 1, spread)
+
+    def back_index(c, j):
+        if isinstance(c, int):
+            if c == 0:
+                return (j + 2) % 4
+            return 2 * c + j if j >= 2 else 2 + 2 * chunks + 2 * c + j
+        later = jnp.where(j >= 2, 2 * c + j, 2 + 2 * chunks + 2 * c + j)
+        return jnp.where(c == 0, lax.rem(j + 2, 4), later)
 
     even = lax.broadcasted_iota(jnp.int32, (rows, HEAD_DIM), 1) % 2 == 0
 
@@ -580,6 +619,21 @@
             "width", target,
         )
 
+    def back_arrived(side, p):
+        copy(
+            back.at[side, p], back.at[side, p], back_send.at[side, p], back_recv.at[side, p],
+            "width", inner,
+        ).wait_recv()
+
+    def drain(i):
+        back_arrived(0, i)
+        back_across(i).start()
+        relay_home(pieces - LAG + i)
+
+    @pl.when(is_mid)
+    def _():
+        loop(LAG, drain)
+
     outer_core = copy(outer, outer_got.at[0], outer_send.at[0], outer_recv.at[0], "ffn", core_peer)
     outer_chip = copy(outer_pair, outer_got.at[1], outer_send.at[1], outer_recv.at[1], "ffn", chip_peer)
 
@@ -588,6 +642,7 @@
         low_copy(0, 0, inner).wait_recv()
         low[...] = (low_own[...] + low_got[0].astype(f32)).astype(bf16)
         outer[...] = jnp.zeros_like(outer)
+        misc[0] = jnp.zeros(misc.shape[1:], f32)
         key_grad[...] = jnp.zeros_like(key_grad)
         value_grad[...] = jnp.zeros_like(value_grad)
         head_col = pl.multiple_of(half * HEAD_DIM, HEAD_DIM)
@@ -605,85 +660,91 @@
             key_state[pl.ds(start, rows), :] = turned(key_sum, start, 1.0).astype(bf16)
             value_state[pl.ds(start, rows), :] = value_sum.astype(bf16)
 
-        def heads(c):
-            for j in range(4):
-                for kind in (1, 2):
-                    arrived(0, piece_of(kind, c, j))
+        def block_of_head(c, j, head, block):
+            lane = pl.multiple_of(head * HEAD_DIM, HEAD_DIM)
+            lanes = pl.ds(lane, HEAD_DIM)
+            first = pl.multiple_of(half * side_cols + c * cols + lane, HEAD_DIM)
+            query_map = query_up[:, pl.ds(first, HEAD_DIM)]
+            grad_map = output_down[:, pl.ds(first, HEAD_DIM)]
+            start, stop = block * rows, (block + 1) * rows
+            s_q, s_g = piece_of(1, c, j), piece_of(2, c, j)
+            query_sum = buf[0, s_q, :, lanes].astype(f32) + own[s_q, :, lanes].astype(f32)
+            query_sum += adapter_scale * dot(low[j, :rank], query_map, FIRST)
+            query = turned(query_sum, start, 1.0).astype(bf16)
+            grad_sum = buf[0, s_g, :, lanes].astype(f32) + own[s_g, :, lanes].astype(f32)
+            out_rank = low[j, 3 * rank :]
+            grad = (grad_sum + adapter_scale * dot(out_rank, grad_map, FIRST)).astype(bf16)
+            key_part = key_state[:stop, :]
+            value_part = value_state[:stop, :]
+            scores = dot(query, key_part, LAST) * score_scale
+            row = start + lax.broadcasted_iota(jnp.int32, (rows, stop), 0)
+            column = lax.broadcasted_iota(jnp.int32, (rows, stop), 1)
+            scores = jnp.where(row >= column, scores, -jnp.inf)
+            shifted = jnp.exp(scores - jnp.max(scores, axis=1, keepdims=True))
+            probs = shifted * (1.0 / jnp.sum(shifted, axis=1, keepdims=True))
+            weights = probs.astype(bf16)
+            attended = dot(weights, value_part).astype(bf16)
+            outer[j] += dot(grad_map, attended, LAST)
+            misc[0, 4 + c, :, lanes] += adapter_scale * dot(out_rank, attended)
+            prob_grad = dot(grad, value_part, LAST)
+            delta = jnp.sum(grad.astype(f32) * attended.astype(f32), axis=1, keepdims=True)
+            score_grad = (probs * ((prob_grad - delta) * score_scale)).astype(bf16)
+            turned_grad = turned(dot(score_grad, key_part), start, -1.0)
+            back[0, back_index(c, j), :, lanes] = turned_grad.astype(bf16)
+            key_grad[:stop, :] += dot(score_grad, query, FIRST)
+            value_grad[:stop, :] += dot(weights, grad, FIRST)
+
+        def attend(i):
+            c = lax.div(i, 4)
+            j = lax.rem(i + 2, 4)
+            arrived(0, piece_of(1, c, j))
+            arrived(0, piece_of(2, c, j))
+            here = other_index(f, j)
 
             def one_head(head):
-                lane = pl.multiple_of(head * HEAD_DIM, HEAD_DIM)
-                lanes = pl.ds(lane, HEAD_DIM)
-                first = pl.multiple_of(half * side_cols + c * cols + lane, HEAD_DIM)
-                query_map = query_up[:, pl.ds(first, HEAD_DIM)]
-                grad_map = output_down[:, pl.ds(first, HEAD_DIM)]
-                map_grad = jnp.zeros((rank, HEAD_DIM), f32)
                 for block in range(BLOCKS):
-                    start, stop = block * rows, (block + 1) * rows
-                    j = other_index(f, block)
-                    near = j < 2
-                    base = 2 + 4 * chunks
-                    s_q = jnp.where(near, 2 + 2 * c + j, base + 2 + 4 * c + 2 * (j - 2))
-                    s_g = jnp.where(near, 2 + 2 * chunks + 2 * c + j, base + 3 + 4 * c + 2 * (j - 2))
-                    query_sum = buf[0, s_q, :, lanes].astype(f32) + own[s_q, :, lanes].astype(f32)
-                    query_sum += adapter_scale * dot(low[j, :rank], query_map, FIRST)
-                    query = turned(query_sum, start, 1.0).astype(bf16)
-                    grad_sum = buf[0, s_g, :, lanes].astype(f32) + own[s_g, :, lanes].astype(f32)
-                    out_rank = low[j, 3 * rank :]
-                    grad = (grad_sum + adapter_scale * dot(out_rank, grad_map, FIRST)).astype(bf16)
-                    key_part = key_state[:stop, :]
-                    value_part = value_state[:stop, :]
-                    scores = dot(query, key_part, LAST) * score_scale
-                    row = start + lax.broadcasted_iota(jnp.int32, (rows, stop), 0)
-                    column = lax.broadcasted_iota(jnp.int32, (rows, stop), 1)
-                    scores = jnp.where(row >= column, scores, -jnp.inf)
-                    shifted = jnp.exp(scores - jnp.max(scores, axis=1, keepdims=True))
-                    probs = shifted * (1.0 / jnp.sum(shifted, axis=1, keepdims=True))
-                    weights = probs.astype(bf16)
-                    attended = dot(weights, value_part).astype(bf16)
-                    outer[j] += dot(grad_map, attended, LAST)
-                    map_grad += dot(out_rank, attended)
-                    prob_grad = dot(grad, value_part, LAST)
-                    delta = jnp.sum(
-                        grad.astype(f32) * attended.astype(f32), axis=1, keepdims=True
+                    pl.when(here == block)(
+                        functools.partial(block_of_head, c, j, head, block)
                     )
-                    score_grad = (probs * ((prob_grad - delta) * score_scale)).astype(bf16)
-                    p = 4 * c + lax.rem(j + 2, 4)
-                    back[0, p, :, lanes] = turned(dot(score_grad, key_part), start, -1.0).astype(bf16)
-                    key_grad[:stop, :] += dot(score_grad, query, FIRST)
-                    value_grad[:stop, :] += dot(weights, grad, FIRST)
-                misc[0, 4 + c, :, lanes] = adapter_scale * map_grad
 
             loop(CHUNK_HEADS, one_head)
-            for k in range(4):
-                back_home(4 * c + k).start()
-
-        loop(chunks, heads)
+
+            @pl.when((c == 0) | (j >= 2))
+            def _():
+                back_home(back_index(c, j)).start()
+
+        loop(4 * chunks, attend)
         outer_core.start()
+
+        def send_key_value(j):
+            p = back_index(chunks, j)
+            start = pl.multiple_of(other_index(f, j) * rows, rows)
+            key_block = turned(key_grad[pl.ds(start, rows), :], start, -1.0)
+            back[0, p, :, :HEAD_DIM] = key_block.astype(bf16)
+            back[0, p, :, HEAD_DIM:] = value_grad[pl.ds(start, rows), :].astype(bf16)
+            back_home(p).start()
+
+        send_key_value(2)
+        send_key_value(3)
+        for c in range(1, chunks):
+            for j in range(2):
+                back_home(back_index(c, j)).start()
         outer_core.wait_recv()
         for j in range(4):
             outer_pair[j] = outer[j] + outer_got[0, j + 1 - 2 * (j % 2)]
         outer_chip.start()
-        for k in range(4):
-            j = (k + 2) % 4
-            start = pl.multiple_of(other_index(f, j) * rows, rows)
-            key_block = turned(key_grad[pl.ds(start, rows), :], start, -1.0)
-            back[0, 4 * chunks + k, :, :HEAD_DIM] = key_block.astype(bf16)
-            back[0, 4 * chunks + k, :, HEAD_DIM:] = value_grad[pl.ds(start, rows), :].astype(bf16)
-            back_home(4 * chunks + k).start()
         outer_chip.wait_recv()
         for j in range(4):
             misc[0, j] = outer_pair[j] + outer_got[1, (j + 2) % 4]
         misc_copy(0, 0, inner).start()
-
-    def back_arrived(side, p):
-        copy(
-            back.at[side, p], back.at[side, p], back_send.at[side, p], back_recv.at[side, p],
-            "width", inner,
-        ).wait_recv()
+        send_key_value(0)
+        send_key_value(1)
 
     def absorb(side, p):
-        c = lax.div(p, 4)
-        j = lax.rem(lax.rem(p, 4) + 2, 4)
+        late = p >= far_back
+        r = jnp.maximum(p - jnp.where(late, far_back, 4), 0)
+        c = jnp.where(p < 4, 0, 1 + lax.div(r, 2))
+        j = jnp.where(p < 4, lax.rem(p + 2, 4), lax.rem(r, 2) + jnp.where(late, 0, 2))
         step = min(2 * cols, width)
         for n in range(width // step):
             at = slice(n * step, (n + 1) * step)
@@ -704,29 +765,6 @@
                 at = slice((i + 1) * rank, (i + 2) * rank)
                 rank_sum[j, at] += dot(key_value_up[i, :, pl.ds(column, HEAD_DIM)], values, LAST)
                 key_value_acc[which, i] += dot(low[j, at], values)
-
-    def back_step(t):
-        @pl.when((t < back_pieces) & is_mid)
-        def _():
-            back_arrived(0, t)
-            back_across(t).start()
-
-        @pl.when(t >= BACK_LAG)
-        def _():
-            back_arrived(1, t - BACK_LAG)
-
-            @pl.when(is_mid)
-            def _():
-                back_out(t - BACK_LAG).start()
-
-        def absorb_side(side):
-            p = t - BACK_LAG * side
-
-            @pl.when((p >= 0) & (p < back_pieces))
-            def _():
-                absorb(side, p)
-
-        loop(2, absorb_side)
 
     def land_copy(first, count, slot, at, sem, axis, target):
         return copy(
@@ -743,44 +781,62 @@
         for n in range(parts)
     ]
 
-    @pl.when(is_mid)
-    def _():
-        loop(pieces, lambda s: send_home(s).wait_send())
-
-    loop(back_pieces - 2 + BACK_LAG, back_step)
-    for n in range(tiles):
-        own[n] = acc[3, :, n * cols : (n + 1) * cols].astype(bf16)
-    far_pair.start()
-    loop(back_pieces + BACK_LAG, back_step, back_pieces - 2 + BACK_LAG)
-    far_pair.wait_recv()
-    for n in range(tiles):
-        pair = acc[2, :, n * cols : (n + 1) * cols] + land[1, n].astype(f32)
-        own[2 * tiles + n] = pair.astype(bf16)
-    for part in chip_parts[: parts // 2]:
-        part.start()
-    rank_core = copy(rank_sum, rank_got.at[0], rank_send.at[0], rank_recv.at[0], "ffn", core_peer)
-    rank_chip = copy(rank_pair, rank_got.at[1], rank_send.at[1], rank_recv.at[1], "ffn", chip_peer)
+    def back_step(t):
+        @pl.when((t == back_pieces - 2 - LAG) & is_mid)
+        def _():
+            misc_copy(0, 0, inner).wait_recv()
+            misc_copy(0, 1, inner).start()
+
+        @pl.when((t + LAG < back_pieces) & is_mid)
+        def _():
+            back_arrived(0, t + LAG)
+            back_across(t + LAG).start()
+
+        @pl.when(t == back_pieces - 2)
+        def _():
+            misc_copy(1, 1, inner).wait_recv()
+
+        @pl.when((t == back_pieces - 2) & is_mid)
+        def _():
+            misc_copy(1, 1, outward).start()
+
+        back_arrived(1, t)
+
+        @pl.when(is_mid)
+        def _():
+            back_out(t).start()
+
+        loop(2, lambda side: absorb(side, t))
+
+        @pl.when(t == far_back - 1)
+        def _():
+            for n in range(tiles):
+                own[n] = acc[3, :, n * cols : (n + 1) * cols].astype(bf16)
+            far_pair.start()
+
+        @pl.when(t == far_back + 1)
+        def _():
+            far_pair.wait_recv()
+            for n in range(tiles):
+                pair = acc[2, :, n * cols : (n + 1) * cols] + land[1, n].astype(f32)
+                own[2 * tiles + n] = pair.astype(bf16)
+            for part in chip_parts:
+                part.start()
+
+    loop(back_pieces, back_step)
+    rank_core = copy(rank_sum, rank_got, rank_send.at[0], rank_recv.at[0], "ffn", core_peer)
+    rank_chip = copy(rank_pair, rank_far, rank_send.at[1], rank_recv.at[1], "ffn", chip_peer)
     rank_core.start()
     for n in range(tiles):
         own[tiles + n] = acc[1, :, n * cols : (n + 1) * cols].astype(bf16)
     near_pair.start()
     rank_core.wait_recv()
     for j in range(4):
-        rank_pair[j] = rank_sum[j] + rank_got[0, j + 1 - 2 * (j % 2)]
+        rank_pair[j] = (rank_sum[j] + rank_got[j + 1 - 2 * (j % 2)]).astype(bf16)
     rank_chip.start()
-    for part in chip_parts[parts // 2 :]:
-        part.start()
-
-    @pl.when(is_mid)
-    def _():
-        misc_copy(0, 0, inner).wait_recv()
-        misc_copy(0, 1, inner).start()
-        misc_copy(1, 1, outward).wait_recv()
-        misc_copy(1, 1, outward).start()
-
-    @pl.when(is_end)
-    def _():
-        misc_copy(1, 1, inner).wait_recv()
+
+    def put(n):
+        return pltpu.make_async_copy(staged[n], results[n], result_sem.at[n])
 
     outer_rank = [(misc[0, j] + misc[1, j]).astype(bf16) for j in range(4)]
     for side in range(2):
@@ -797,21 +853,37 @@
     for j in range(1, 4):
         total += dot(outer_rank[j], up[j])
     output_up_out[...] = adapter_scale * total
+    for n in range(2, 6):
+        put(n).start()
+    near_pair.wait_recv()
+    for n in range(tiles):
+        at = slice(n * cols, (n + 1) * cols)
+        acc[0, :, at] += land[0, n].astype(f32)
     rank_chip.wait_recv()
-    ranks = [(rank_pair[j] + rank_got[1, (j + 2) % 4]).astype(bf16) for j in range(4)]
+    ranks = [
+        (rank_pair[j].astype(f32) + rank_far[(j + 2) % 4].astype(f32)).astype(bf16) for j in range(4)
+    ]
     total = dot(ranks[0], hid[0])
     for j in range(1, 4):
         total += dot(ranks[j], hid[j])
     down_out[...] = adapter_scale * total
-    near_pair.wait_recv()
-    for n in range(tiles):
-        at = slice(n * cols, (n + 1) * cols)
-        acc[0, :, at] += land[0, n].astype(f32) + adapter_scale * dot(ranks[0], down[:, at], FIRST)
+    put(1).start()
+    part_cols = per_part * cols
+    put_parts = [
+        pltpu.make_async_copy(
+            hidden_out.at[:, pl.ds(n * part_cols, part_cols)],
+            results[0].at[:, pl.ds(n * part_cols, part_cols)],
+            result_sem.at[6 + n],
+        )
+        for n in range(parts)
+    ]
     for part_index, part in enumerate(chip_parts):
         part.wait_recv()
         for n in range(part_index * per_part, (part_index + 1) * per_part):
             at = slice(n * cols, (n + 1) * cols)
-            hidden_out[:, at] = (acc[0, :, at] + land[2, n].astype(f32)).astype(bf16)
+            adapter = adapter_scale * dot(ranks[0], down[:, at], FIRST)
+            hidden_out[:, at] = (acc[0, :, at] + land[2, n].astype(f32) + adapter).astype(bf16)
+        put_parts[part_index].start()
 
     for which in range(2):
         for kind in range(3):
@@ -823,6 +895,7 @@
 
     @pl.when(is_mid)
     def _():
+        loop(pieces, lambda s: send_home(s).wait_send())
         loop(back_pieces, lambda p: back_out(p).wait_send())
         low_copy(1, 0, outward).wait_send()
         misc_copy(1, 1, outward).wait_send()
@@ -838,6 +911,25 @@
         part.wait_send()
     rank_core.wait_send()
     rank_chip.wait_send()
+    for n in range(1, 6):
+        put(n).wait()
+    for part in put_parts:
+        part.wait()
+
+
+def pass_on(*refs):
+    count = (len(refs) - 2) // 3
+    sources, results, held = refs[:count], refs[count : 2 * count], refs[2 * count : 3 * count]
+    in_sem, out_sem = refs[3 * count :]
+    fetch = [pltpu.make_async_copy(s, h, in_sem.at[n]) for n, (s, h) in enumerate(zip(sources, held))]
+    store = [pltpu.make_async_copy(h, r, out_sem.at[n]) for n, (h, r) in enumerate(zip(held, results))]
+    for copy in fetch:
+        copy.start()
+    for arrived, copy in zip(fetch, store):
+        arrived.wait()
+        copy.start()
+    for copy in store:
+        copy.wait()
 
 
 def one_kernel(
@@ -867,23 +959,35 @@
     angles = np.arange(tokens)[:, None] * frequency[None, :]
     cosine = jnp.asarray(np.cos(angles), f32)
     sine = jnp.asarray(np.sin(angles), f32)
-    vmem = pl.BlockSpec(memory_space=pltpu.VMEM)
     hbm = pl.BlockSpec(memory_space=pl.ANY)
     dma = pltpu.SemaphoreType.DMA
     shape = jax.ShapeDtypeStruct
+    results = (
+        shape((rows, width), bf16),
+        shape((3 * rank, width), f32),
+        shape(query_up_map.shape, f32),
+        shape(key_value_up_maps.shape, f32),
+        shape(output_down_map.shape, f32),
+        shape(output_up.shape, f32),
+    )
+    held = [pltpu.VMEM(result.shape, result.dtype) for result in results]
+    small = (
+        cosine,
+        sine,
+        adapter_down.reshape(3 * rank, width),
+        query_up_map,
+        key_value_up_maps,
+        output_down_map,
+        output_up,
+    )
     outputs = pl.pallas_call(
         functools.partial(fused, 1.0 / math.sqrt(HEAD_DIM)),
-        out_shape=(
-            shape((rows, width), bf16),
-            shape((3 * rank, width), f32),
-            shape(query_up_map.shape, f32),
-            shape(key_value_up_maps.shape, f32),
-            shape(output_down_map.shape, f32),
-            shape(output_up.shape, f32),
-        ),
-        in_specs=[hbm] * 5 + [vmem] * 7,
-        out_specs=(vmem,) * 6,
+        out_shape=results,
+        in_specs=[hbm] * 12,
+        out_specs=(hbm,) * 6,
         scratch_shapes=[
+            *[pltpu.VMEM(array.shape, array.dtype) for array in small],
+            *held,
             pltpu.VMEM((4, rows, width), bf16),
             pltpu.VMEM((4, rows, width), bf16),
             pltpu.VMEM((2, chunks + 1, width, cols), bf16),
@@ -903,8 +1007,9 @@
             pltpu.VMEM((2, 4, 4 * rank, rows), bf16),
             pltpu.VMEM((4, 4 * rank, rows), bf16),
             pltpu.VMEM((4, 3 * rank, rows), f32),
+            pltpu.VMEM((4, 3 * rank, rows), bf16),
             pltpu.VMEM((4, 3 * rank, rows), f32),
-            pltpu.VMEM((2, 4, 3 * rank, rows), f32),
+            pltpu.VMEM((4, 3 * rank, rows), bf16),
             pltpu.VMEM((4, rank, rows), f32),
             pltpu.VMEM((4, rank, rows), f32),
             pltpu.VMEM((2, 4, rank, rows), f32),
@@ -930,6 +1035,8 @@
             dma((6,)),
             dma((2,)),
             dma((2,)),
+            dma((7,)),
+            dma((10,)),
         ],
         compiler_params=pltpu.CompilerParams(
             collective_id=0, has_side_effects=True, vmem_limit_bytes=67_000_000
@@ -940,14 +1047,15 @@
         query_frozen_weight,
         key_value_frozen_weight,
         output_frozen_weight,
-        cosine,
-        sine,
-        adapter_down.reshape(3 * rank, width),
-        query_up_map,
-        key_value_up_maps,
-        output_down_map,
-        output_up,
-    )
+        *small,
+    )
+    outputs = pl.pallas_call(
+        pass_on,
+        out_shape=results,
+        in_specs=[hbm] * 6,
+        out_specs=(hbm,) * 6,
+        scratch_shapes=[*held, dma((6,)), dma((6,))],
+    )(*outputs)
     return (outputs[0], outputs[1].reshape(adapter_down.shape), *outputs[2:])
 
 
@@ -959,6 +1067,7 @@
         and lax.axis_size("width") == 4
         and lax.axis_size("ffn") == 4
         and arrays[2].shape[1] % (2 * cols) == 0
+        and arrays[2].shape[1] >= 6 * cols
         and rows == cols
         and width % (4 * cols) == 0
     )

time: 239 us -> 201 us (0.84)
  Pallas kernels: 228 us -> 200 us
  local copies, waits for them, and re-layouts: 10.1 us -> 0 us
    pallas_call x1, Pallas kernels: 228 us -> 198 us  [one_kernel(): pl.pallas_call(functools.partial(fused, 1.0 / math.sqrt(HEAD_DIM)), out_s...]
    unnamed x6 -> x0, local copies, waits for them, and re-layouts: 10.1 us -> none
    pallas_call x0 -> x1, Pallas kernels: none -> 2.56 us  [one_kernel(): pl.pallas_call(pass_on, out_shape=results, in_specs=[hbm] * 6, out_specs=...]
where the time goes in v2:
time: 201 us
  Pallas kernels  200 us (100%)
    pallas_call x1, Pallas kernels, one_kernel(): pl.pallas_call(functools.partial(fused, 1.0 / math.sqrt(HEAD_DIM)), out_s...  198 us

profile of v2, /device:TPU:0, one launch (start us, length us, event | category | flops | bytes accessed | tf_op | source)
XLA Modules:
  0.0 201.0 jit_solution(4804141971191361470)
XLA Ops:
  0.6 197.8 %shard_map.163 = (bf16[256,2048]{1,0:T(8,128)(2,1)}, f32[48,2048]{1,0:T(8,128)}, f32[16,2048]{1,0:T(8,128)}, f32[2,16,256]{2,1,0:T(8,128)}, f32[16,2048]{1,0:T(8,128)}, /*index=5*/f32[16,2048]{1,0:T(8,128)}) custom-call(bf16[256,2048]{1,0:T(8,128)(2,1)} %hidden_in.1, bf16[256,2048]{1,0:T(8,128)(2,1)} %upstream_in.1, bf16[2048,2048]{1,0:T(8,128)(2,1)} %query_weight.1, ...), custom_call_target="tpu_custom_call" | custom-call | tf_op jit(solution)/shard_map/pallas_call | solution.py:983
  198.4 2.6 %shard_map.164 = (bf16[256,2048]{1,0:T(8,128)(2,1)}, f32[48,2048]{1,0:T(8,128)}, f32[16,2048]{1,0:T(8,128)}, f32[2,16,256]{2,1,0:T(8,128)}, f32[16,2048]{1,0:T(8,128)}, /*index=5*/f32[16,2048]{1,0:T(8,128)}) custom-call(bf16[256,2048]{1,0:T(8,128)(2,1)} %get-tuple-element.18.refs_0_, f32[48,2048]{1,0:T(8,128)} %get-tuple-element.19.refs_1_, ...), custom_call_target="tpu_custom_call" | custom-call | tf_op jit(solution)/shard_map/pallas_call | solution.py:1052

commit v3 on v2

--- a/solution.py
+++ b/solution.py
@@ -14,7 +14,7 @@
 ADAPTER_RANK = 16
 CHUNK_HEADS = 2
 BLOCKS = 4
-LAG = 3
+LAG = 4
 MESH = pl.DeviceIdType.MESH
 LAST = (((1,), (1,)), ((), ()))
 FIRST = (((0,), (0,)), ((), ()))
@@ -275,6 +275,14 @@
     return 2 * high + low
 
 
+def block_at(k):
+    return jnp.where(k < 2, 3 - k, k - 2)
+
+
+def place_of(j):
+    return jnp.where(j < 2, j + 2, 3 - j)
+
+
 def fused(
     score_scale,
     hidden_in, upstream_in, query_weight, key_value_weight, output_weight,
@@ -284,7 +292,7 @@
     (
         hid, up, wh, wg, buf, own, back, acc, land, tmp, key_state, value_state, key_grad, value_grad,
         low_own, low_sent, low_got, low, rank_sum, rank_pair, rank_got, rank_far, outer, outer_pair,
-        outer_got, misc, query_acc, key_value_acc,
+        outer_got, misc, passed, query_acc, key_value_acc,
         load_sem, weight_sem, grad_sem, gather_send, gather_recv, send_sem, recv_sem, back_send,
         back_recv, low_send, low_recv, misc_send, misc_recv, outer_send, outer_recv, land_send,
         land_recv, rank_send, rank_recv, small_sem, result_sem,
@@ -304,6 +312,7 @@
     far_back = 4 + 2 * chunks
     back_pieces = 4 + 4 * chunks
     tiles = width // cols
+    half_rows = rows // 2
     f = lax.axis_index("ffn")
     z = lax.axis_index("width")
     half = lax.div(z, 2)
@@ -403,50 +412,69 @@
     for load in load_small:
         load.start()
 
-    def send_away_end(s):
-        return copy(buf.at[1, s], buf.at[1, s], send_sem.at[1, s], recv_sem.at[1, s], "width", inner)
-
-    def send_away_mid(s):
-        return copy(buf.at[1, s], buf.at[0, s], send_sem.at[1, s], recv_sem.at[0, s], "width", inner)
-
-    def send_home(s):
-        return copy(buf.at[0, s], buf.at[0, s], send_sem.at[0, s], recv_sem.at[0, s], "width", outward)
-
-    def arrived(side, s):
-        copy(
-            buf.at[side, s], buf.at[side, s], send_sem.at[side, s], recv_sem.at[side, s], "width", inner
-        ).wait_recv()
-
-    def relay_home(s):
-        arrived(0, s)
-        buf[0, s] = (buf[0, s].astype(f32) + own[s].astype(f32)).astype(bf16)
-        send_home(s).start()
+    def half_of(ref, side, u):
+        start = pl.multiple_of(lax.rem(u, 2) * half_rows, half_rows)
+        return ref.at[side, lax.div(u, 2), pl.ds(start, half_rows)]
+
+    def send_away_end(u):
+        part = half_of(buf, 1, u)
+        return copy(part, part, send_sem.at[1], recv_sem.at[1, u], "width", inner)
+
+    def send_away_mid(u):
+        return copy(
+            half_of(buf, 1, u), half_of(buf, 0, u), send_sem.at[1], recv_sem.at[0, u], "width", inner
+        )
+
+    def send_home(u):
+        part = half_of(buf, 0, u)
+        return copy(part, part, send_sem.at[0], recv_sem.at[0, u], "width", outward)
+
+    def arrived(side, u):
+        part = half_of(buf, side, u)
+        copy(part, part, send_sem.at[side], recv_sem.at[side, u], "width", inner).wait_recv()
+
+    def piece_arrived(s):
+        arrived(0, 2 * s)
+        arrived(0, 2 * s + 1)
+
+    def relay_home(u):
+        s = lax.div(u, 2)
+        at = pl.ds(pl.multiple_of(lax.rem(u, 2) * half_rows, half_rows), half_rows)
+        arrived(0, u)
+        buf[0, s, at] = (buf[0, s, at].astype(f32) + own[s, at].astype(f32)).astype(bf16)
+        send_home(u).start()
 
     def push(s):
         @pl.when(is_end)
         def _():
             buf[1, s] = tmp[...].astype(bf16)
-            send_away_end(s).start()
+            for h in range(2):
+                send_away_end(2 * s + h).start()
 
         @pl.when(is_mid)
         def _():
-            arrived(1, s)
-            buf[1, s] = (buf[1, s].astype(f32) + tmp[...]).astype(bf16)
-            send_away_mid(s).start()
-
-            @pl.when(s >= LAG)
-            def _():
-                relay_home(s - LAG)
+            def one_half(h):
+                u = 2 * s + h
+                at = pl.ds(pl.multiple_of(h * half_rows, half_rows), half_rows)
+                arrived(1, u)
+                buf[1, s, at] = (buf[1, s, at].astype(f32) + tmp[at, :]).astype(bf16)
+                send_away_mid(u).start()
+
+                @pl.when(u >= LAG)
+                def _():
+                    relay_home(u - LAG)
+
+            loop(2, one_half)
 
     def hidden_step(s, c, j):
         tmp[...] = dot(hid[j], wh[1, c])
+        push(s)
         own[s] = dot(hid[j], wh[0, c]).astype(bf16)
-        push(s)
 
     def upstream_step(s, slot, j):
         tmp[...] = dot(up[j], wg[slot, 1], LAST)
+        push(s)
         own[s] = dot(up[j], wg[slot, 0], LAST).astype(bf16)
-        push(s)
 
     def wait_grad_weight(fetch):
         for side in range(2):
@@ -484,7 +512,7 @@
         grad = jnp.where(in_last, lax.rem(tail, 2), lax.div(quarter, 2))
         is_grad = (grad == 1) & (r >= 0)
         j = jnp.where(key_value, r + 2, lax.rem(quarter, 2)) + jnp.where(late, 2, 0)
-        j = jnp.where(in_last, lax.rem(lax.div(tail, 2) + 2, 4), j)
+        j = jnp.where(in_last, block_at(lax.div(tail, 2)), j)
         fetch = jnp.where(in_last, 2 * last, c + jnp.where(late, last, 0))
 
         @pl.when(s == 1)
@@ -550,7 +578,7 @@
             low_sent[0] = (low_own[...] + low_got[1].astype(f32)).astype(bf16)
             low_copy(0, 0, inner).start()
 
-        @pl.when((s == near_end + 6 + LAG) & is_mid)
+        @pl.when((s == near_end + 8) & is_mid)
         def _():
             low_copy(1, 0, outward).wait_recv()
             total = low_own[...] + low_got[0].astype(f32)
@@ -585,15 +613,13 @@
         if kind == 0:
             return j if j < 2 else near_end + j - 2
         spread = jnp.where(j < 2, 2 + j, near_end + j) + 4 * c + 2 * (kind - 1)
-        return jnp.where(c == last, far_end + 2 * lax.rem(j + 2, 4) + kind - 1, spread)
+        return jnp.where(c == last, far_end + 2 * place_of(j) + kind - 1, spread)
 
     def back_index(c, j):
         if isinstance(c, int):
-            if c == 0:
-                return (j + 2) % 4
-            return 2 * c + j if j >= 2 else 2 + 2 * chunks + 2 * c + j
-        later = jnp.where(j >= 2, 2 * c + j, 2 + 2 * chunks + 2 * c + j)
-        return jnp.where(c == 0, lax.rem(j + 2, 4), later)
+            return 2 * c + 5 - j if j >= 2 else 2 + 2 * chunks + 2 * c + j
+        later = jnp.where(j >= 2, 2 * c + 5 - j, 2 + 2 * chunks + 2 * c + j)
+        return jnp.where(c == 0, place_of(j), later)
 
     even = lax.broadcasted_iota(jnp.int32, (rows, HEAD_DIM), 1) % 2 == 0
 
@@ -604,31 +630,37 @@
         at = pl.ds(start, rows)
         return values * cosine[at, :] + direction * partner * sine[at, :]
 
-    def back_home(p):
-        return copy(back.at[0, p], back.at[0, p], back_send.at[0, p], back_recv.at[0, p], "width", inner)
-
-    def back_across(p):
-        return copy(back.at[0, p], back.at[1, p], back_send.at[0, p], back_recv.at[1, p], "width", inner)
-
-    def back_out(p):
-        return copy(back.at[1, p], back.at[1, p], back_send.at[1, p], back_recv.at[1, p], "width", outward)
+    def back_home(v):
+        part = half_of(back, 0, v)
+        return copy(part, part, back_send.at[0], back_recv.at[0, v], "width", inner)
+
+    def back_across(v):
+        return copy(
+            half_of(back, 0, v), half_of(back, 1, v), back_send.at[0], back_recv.at[1, v], "width", inner
+        )
+
+    def back_out(v):
+        part = half_of(back, 1, v)
+        return copy(part, part, back_send.at[1], back_recv.at[1, v], "width", outward)
+
+    def send_back(p):
+        for h in range(2):
+            back_home(2 * p + h).start()
 
     def misc_copy(slot, target_slot, target):
         return copy(
-            misc.at[slot], misc.at[target_slot], misc_send.at[slot], misc_recv.at[target_slot],
+            passed.at[slot], passed.at[target_slot], misc_send.at[slot], misc_recv.at[target_slot],
             "width", target,
         )
 
-    def back_arrived(side, p):
-        copy(
-            back.at[side, p], back.at[side, p], back_send.at[side, p], back_recv.at[side, p],
-            "width", inner,
-        ).wait_recv()
+    def back_arrived(side, v):
+        part = half_of(back, side, v)
+        copy(part, part, back_send.at[side], back_recv.at[side, v], "width", inner).wait_recv()
 
     def drain(i):
         back_arrived(0, i)
         back_across(i).start()
-        relay_home(pieces - LAG + i)
+        relay_home(2 * pieces - LAG + i)
 
     @pl.when(is_mid)
     def _():
@@ -642,7 +674,7 @@
         low_copy(0, 0, inner).wait_recv()
         low[...] = (low_own[...] + low_got[0].astype(f32)).astype(bf16)
         outer[...] = jnp.zeros_like(outer)
-        misc[0] = jnp.zeros(misc.shape[1:], f32)
+        misc[...] = jnp.zeros_like(misc)
         key_grad[...] = jnp.zeros_like(key_grad)
         value_grad[...] = jnp.zeros_like(value_grad)
         head_col = pl.multiple_of(half * HEAD_DIM, HEAD_DIM)
@@ -650,7 +682,7 @@
         value_map = key_value_up[1, :, pl.ds(head_col, HEAD_DIM)]
         for j in range(4):
             s = piece_of(0, 0, j)
-            arrived(0, s)
+            piece_arrived(s)
             start = pl.multiple_of(other_index(f, j) * rows, rows)
             total = buf[0, s].astype(f32) + own[s].astype(f32)
             key_sum = total[:, :HEAD_DIM] + adapter_scale * dot(low[j, rank : 2 * rank], key_map, FIRST)
@@ -685,7 +717,7 @@
             weights = probs.astype(bf16)
             attended = dot(weights, value_part).astype(bf16)
             outer[j] += dot(grad_map, attended, LAST)
-            misc[0, 4 + c, :, lanes] += adapter_scale * dot(out_rank, attended)
+            misc[c, :, lanes] += adapter_scale * dot(out_rank, attended)
             prob_grad = dot(grad, value_part, LAST)
             delta = jnp.sum(grad.astype(f32) * attended.astype(f32), axis=1, keepdims=True)
             score_grad = (probs * ((prob_grad - delta) * score_scale)).astype(bf16)
@@ -696,9 +728,9 @@
 
         def attend(i):
             c = lax.div(i, 4)
-            j = lax.rem(i + 2, 4)
-            arrived(0, piece_of(1, c, j))
-            arrived(0, piece_of(2, c, j))
+            j = block_at(lax.rem(i, 4))
+            piece_arrived(piece_of(1, c, j))
+            piece_arrived(piece_of(2, c, j))
             here = other_index(f, j)
 
             def one_head(head):
@@ -711,7 +743,7 @@
 
             @pl.when((c == 0) | (j >= 2))
             def _():
-                back_home(back_index(c, j)).start()
+                send_back(back_index(c, j))
 
         loop(4 * chunks, attend)
         outer_core.start()
@@ -722,29 +754,32 @@
             key_block = turned(key_grad[pl.ds(start, rows), :], start, -1.0)
             back[0, p, :, :HEAD_DIM] = key_block.astype(bf16)
             back[0, p, :, HEAD_DIM:] = value_grad[pl.ds(start, rows), :].astype(bf16)
-            back_home(p).start()
-
+            send_back(p)
+
+        send_key_value(3)
         send_key_value(2)
-        send_key_value(3)
         for c in range(1, chunks):
             for j in range(2):
-                back_home(back_index(c, j)).start()
+                send_back(back_index(c, j))
+        send_key_value(0)
+        send_key_value(1)
         outer_core.wait_recv()
         for j in range(4):
             outer_pair[j] = outer[j] + outer_got[0, j + 1 - 2 * (j % 2)]
         outer_chip.start()
         outer_chip.wait_recv()
         for j in range(4):
-            misc[0, j] = outer_pair[j] + outer_got[1, (j + 2) % 4]
+            passed[0, j] = (outer_pair[j] + outer_got[1, (j + 2) % 4]).astype(bf16)
+        for c in range(chunks):
+            passed[0, 4 + c] = misc[c].astype(bf16)
         misc_copy(0, 0, inner).start()
-        send_key_value(0)
-        send_key_value(1)
 
     def absorb(side, p):
         late = p >= far_back
         r = jnp.maximum(p - jnp.where(late, far_back, 4), 0)
         c = jnp.where(p < 4, 0, 1 + lax.div(r, 2))
-        j = jnp.where(p < 4, lax.rem(p + 2, 4), lax.rem(r, 2) + jnp.where(late, 0, 2))
+        j = jnp.where(late, lax.rem(r, 2), 3 - lax.rem(r, 2))
+        j = jnp.where(p < 4, block_at(p), j)
         step = min(2 * cols, width)
         for n in range(width // step):
             at = slice(n * step, (n + 1) * step)
@@ -774,100 +809,157 @@
 
     far_pair = land_copy(0, tiles, 1, 0, 0, "ffn", core_peer)
     near_pair = land_copy(tiles, tiles, 0, 0, 1, "ffn", core_peer)
-    parts = 4
+    parts = tiles
     per_part = tiles // parts
     chip_parts = [
         land_copy(2 * tiles + n * per_part, per_part, 2, n * per_part, 2 + n, "ffn", chip_peer)
         for n in range(parts)
     ]
 
+    def rank_core(first, sem):
+        part = pl.ds(first, 2)
+        return copy(
+            rank_sum.at[part], rank_got.at[part], rank_send.at[sem], rank_recv.at[sem], "ffn", core_peer
+        )
+
+    def rank_chip(first, sem):
+        return copy(
+            rank_pair.at[pl.ds(first, 2)], rank_far.at[pl.ds(2 - first, 2)],
+            rank_send.at[sem], rank_recv.at[sem], "ffn", chip_peer,
+        )
+
+    far_core, far_chip = rank_core(2, 0), rank_chip(2, 1)
+    near_core, near_chip = rank_core(0, 2), rank_chip(0, 3)
+
+    def add_pair(first):
+        for j in (first, first + 1):
+            rank_pair[j] = (rank_sum[j] + rank_got[j + 1 - 2 * (j % 2)]).astype(bf16)
+
     def back_step(t):
-        @pl.when((t == back_pieces - 2 - LAG) & is_mid)
-        def _():
-            misc_copy(0, 0, inner).wait_recv()
-            misc_copy(0, 1, inner).start()
-
-        @pl.when((t + LAG < back_pieces) & is_mid)
-        def _():
-            back_arrived(0, t + LAG)
-            back_across(t + LAG).start()
-
-        @pl.when(t == back_pieces - 2)
-        def _():
-            misc_copy(1, 1, inner).wait_recv()
-
-        @pl.when((t == back_pieces - 2) & is_mid)
-        def _():
-            misc_copy(1, 1, outward).start()
-
-        back_arrived(1, t)
-
-        @pl.when(is_mid)
-        def _():
-            back_out(t).start()
-
+        def relay(h):
+            v = 2 * t + h
+
+            @pl.when((v + LAG < 2 * back_pieces) & is_mid)
+            def _():
+                back_arrived(0, v + LAG)
+                back_across(v + LAG).start()
+
+            @pl.when((v + LAG == 2 * back_pieces) & is_mid)
+            def _():
+                misc_copy(0, 0, inner).wait_recv()
+                misc_copy(0, 1, inner).start()
+
+            back_arrived(1, v)
+
+            @pl.when(is_mid)
+            def _():
+                back_out(v).start()
+
+        loop(2, relay)
         loop(2, lambda side: absorb(side, t))
 
-        @pl.when(t == far_back - 1)
+        @pl.when(t == far_back - 2)
         def _():
             for n in range(tiles):
                 own[n] = acc[3, :, n * cols : (n + 1) * cols].astype(bf16)
             far_pair.start()
 
-        @pl.when(t == far_back + 1)
-        def _():
+        @pl.when(t == far_back - 1)
+        def _():
+            far_core.start()
             far_pair.wait_recv()
             for n in range(tiles):
                 pair = acc[2, :, n * cols : (n + 1) * cols] + land[1, n].astype(f32)
                 own[2 * tiles + n] = pair.astype(bf16)
-            for part in chip_parts:
+            for part in chip_parts[: parts // 2]:
                 part.start()
 
+        @pl.when(t == far_back)
+        def _():
+            far_core.wait_recv()
+            add_pair(2)
+            far_chip.start()
+            for part in chip_parts[parts // 2 : -1]:
+                part.start()
+
     loop(back_pieces, back_step)
-    rank_core = copy(rank_sum, rank_got, rank_send.at[0], rank_recv.at[0], "ffn", core_peer)
-    rank_chip = copy(rank_pair, rank_far, rank_send.at[1], rank_recv.at[1], "ffn", chip_peer)
-    rank_core.start()
+    near_core.start()
     for n in range(tiles):
         own[tiles + n] = acc[1, :, n * cols : (n + 1) * cols].astype(bf16)
     near_pair.start()
-    rank_core.wait_recv()
-    for j in range(4):
-        rank_pair[j] = (rank_sum[j] + rank_got[j + 1 - 2 * (j % 2)]).astype(bf16)
-    rank_chip.start()
+
+    @pl.when(is_mid)
+    def _():
+        misc_copy(1, 1, inner).wait_recv()
+        misc_copy(1, 1, outward).start()
+
+    near_core.wait_recv()
+    add_pair(0)
+    near_chip.start()
+    chip_parts[-1].start()
 
     def put(n):
         return pltpu.make_async_copy(staged[n], results[n], result_sem.at[n])
 
-    outer_rank = [(misc[0, j] + misc[1, j]).astype(bf16) for j in range(4)]
-    for side in range(2):
-        for c in range(chunks):
-            column = pl.multiple_of(side_of(side) * side_cols + c * cols, cols)
-            output_down_out[:, pl.ds(column, cols)] = misc[side, 4 + c]
     for c in range(2 * chunks):
         query_up_out[:, c * cols : (c + 1) * cols] = adapter_scale * query_acc[c]
     for which in range(2):
         for i in range(2):
             at = slice(which * HEAD_DIM, (which + 1) * HEAD_DIM)
             key_value_up_out[i, :, at] = adapter_scale * key_value_acc[which, i]
-    total = dot(outer_rank[0], up[0])
+    put(2).start()
+    put(3).start()
+    far_chip.wait_recv()
+
+    def rank_of(j):
+        return (rank_pair[j].astype(f32) + rank_far[j].astype(f32)).astype(bf16)
+
+    own_ranks = rank_of(0)
+    near_pair.wait_recv()
+    @pl.when(is_end)
+    def _():
+        misc_copy(1, 1, inner).wait_recv()
+
+    for side in range(2):
+        for c in range(chunks):
+            column = pl.multiple_of(side_of(side) * side_cols + c * cols, cols)
+            output_down_out[:, pl.ds(column, cols)] = passed[side, 4 + c].astype(f32)
+    put(4).start()
+
+    def outer_of(j):
+        return (passed[0, j].astype(f32) + passed[1, j].astype(f32)).astype(bf16)
+
+    total = dot(outer_of(0), up[0])
     for j in range(1, 4):
-        total += dot(outer_rank[j], up[j])
+        total += dot(outer_of(j), up[j])
     output_up_out[...] = adapter_scale * total
-    for n in range(2, 6):
-        put(n).start()
-    near_pair.wait_recv()
-    for n in range(tiles):
-        at = slice(n * cols, (n + 1) * cols)
-        acc[0, :, at] += land[0, n].astype(f32)
-    rank_chip.wait_recv()
-    ranks = [
-        (rank_pair[j].astype(f32) + rank_far[(j + 2) % 4].astype(f32)).astype(bf16) for j in range(4)
-    ]
-    total = dot(ranks[0], hid[0])
-    for j in range(1, 4):
-        total += dot(ranks[j], hid[j])
-    down_out[...] = adapter_scale * total
-    put(1).start()
+    put(5).start()
+    for which in range(2):
+        for kind in range(3):
+            gather(which, kind).wait_send()
+
+    def all_sent(ref, side, sem, recv):
+        copy(ref.at[side], ref.at[side], sem.at[side], recv.at[side, 0], "width", inner).wait_send()
+
+    all_sent(buf, 1, send_sem, recv_sem)
+    all_sent(back, 0, back_send, back_recv)
+    low_copy(0, 0, inner).wait_send()
+    misc_copy(0, 0, inner).wait_send()
+
+    @pl.when(is_mid)
+    def _():
+        all_sent(buf, 0, send_sem, recv_sem)
+        all_sent(back, 1, back_send, back_recv)
+        low_copy(1, 0, outward).wait_send()
+        misc_copy(1, 1, outward).wait_send()
+
+    @pl.when(is_end)
+    def _():
+        outer_core.wait_send()
+        outer_chip.wait_send()
+
+    far_pair.wait_send()
+    near_pair.wait_send()
     part_cols = per_part * cols
     put_parts = [
         pltpu.make_async_copy(
@@ -877,40 +969,27 @@
         )
         for n in range(parts)
     ]
-    for part_index, part in enumerate(chip_parts):
-        part.wait_recv()
+
+    def take_part(part_index):
+        chip_parts[part_index].wait_recv()
         for n in range(part_index * per_part, (part_index + 1) * per_part):
             at = slice(n * cols, (n + 1) * cols)
-            adapter = adapter_scale * dot(ranks[0], down[:, at], FIRST)
-            hidden_out[:, at] = (acc[0, :, at] + land[2, n].astype(f32) + adapter).astype(bf16)
+            terms = acc[0, :, at] + land[0, n].astype(f32) + land[2, n].astype(f32)
+            adapter = adapter_scale * dot(own_ranks, down[:, at], FIRST)
+            hidden_out[:, at] = (terms + adapter).astype(bf16)
         put_parts[part_index].start()
 
-    for which in range(2):
-        for kind in range(3):
-            gather(which, kind).wait_send()
-    loop(pieces, lambda s: send_away_end(s).wait_send())
-    loop(back_pieces, lambda p: back_home(p).wait_send())
-    low_copy(0, 0, inner).wait_send()
-    misc_copy(0, 0, inner).wait_send()
-
-    @pl.when(is_mid)
-    def _():
-        loop(pieces, lambda s: send_home(s).wait_send())
-        loop(back_pieces, lambda p: back_out(p).wait_send())
-        low_copy(1, 0, outward).wait_send()
-        misc_copy(1, 1, outward).wait_send()
-
-    @pl.when(is_end)
-    def _():
-        outer_core.wait_send()
-        outer_chip.wait_send()
-
-    far_pair.wait_send()
-    near_pair.wait_send()
-    for part in chip_parts:
+    for part_index in range(parts - 1):
+        take_part(part_index)
+    near_chip.wait_recv()
+    total = dot(own_ranks, hid[0])
+    for j in range(1, 4):
+        total += dot(rank_of(j), hid[j])
+    down_out[...] = adapter_scale * total
+    put(1).start()
+    take_part(parts - 1)
+    for part in (far_core, far_chip, near_core, near_chip, *chip_parts):
         part.wait_send()
-    rank_core.wait_send()
-    rank_chip.wait_send()
     for n in range(1, 6):
         put(n).wait()
     for part in put_parts:
@@ -1013,7 +1092,8 @@
             pltpu.VMEM((4, rank, rows), f32),
             pltpu.VMEM((4, rank, rows), f32),
             pltpu.VMEM((2, 4, rank, rows), f32),
-            pltpu.VMEM((2, 4 + chunks, rank, cols), f32),
+            pltpu.VMEM((chunks, rank, cols), f32),
+            pltpu.VMEM((2, 4 + chunks, rank, cols), bf16),
             pltpu.VMEM((2 * chunks, rank, cols), f32),
             pltpu.VMEM((2, 2, rank, HEAD_DIM), f32),
             dma((2,)),
@@ -1021,22 +1101,22 @@
             dma((2, 2)),
             dma((2, 3)),
             dma((2, 3)),
-            dma((2, pieces)),
-            dma((2, pieces)),
-            dma((2, back_pieces)),
-            dma((2, back_pieces)),
+            dma((2,)),
+            dma((2, 2 * pieces)),
+            dma((2,)),
+            dma((2, 2 * back_pieces)),
             dma((2,)),
             dma((2,)),
             dma((2,)),
             dma((2,)),
             dma((2,)),
             dma((2,)),
-            dma((6,)),
-            dma((6,)),
-            dma((2,)),
-            dma((2,)),
+            dma((2 + tiles,)),
+            dma((2 + tiles,)),
+            dma((4,)),
+            dma((4,)),
             dma((7,)),
-            dma((10,)),
+            dma((6 + tiles,)),
         ],
         compiler_params=pltpu.CompilerParams(
             collective_id=0, has_side_effects=True, vmem_limit_bytes=67_000_000

time: 201 us -> 194 us (0.965)
  Pallas kernels: 200 us -> 193 us
    pallas_call x1, Pallas kernels: 198 us -> 190 us  [one_kernel(): pl.pallas_call(functools.partial(fused, 1.0 / math.sqrt(HEAD_DIM)), out_s...]
where the time goes in v3:
time: 194 us; the launch traced here: 193 us
  Pallas kernels  193 us (99%)
    pallas_call x1, Pallas kernels, one_kernel(): pl.pallas_call(functools.partial(fused, 1.0 / math.sqrt(HEAD_DIM)), out_s...  190 us

profile of v3, /device:TPU:0, one launch (start us, length us, event | category | flops | bytes accessed | tf_op | source)
XLA Modules:
  0.0 193.4 jit_solution(7401870417923171192)
XLA Ops:
  0.6 190.2 %shard_map.163 = (bf16[256,2048]{1,0:T(8,128)(2,1)}, f32[48,2048]{1,0:T(8,128)}, f32[16,2048]{1,0:T(8,128)}, f32[2,16,256]{2,1,0:T(8,128)}, f32[16,2048]{1,0:T(8,128)}, /*index=5*/f32[16,2048]{1,0:T(8,128)}) custom-call(bf16[256,2048]{1,0:T(8,128)(2,1)} %hidden_in.1, bf16[256,2048]{1,0:T(8,128)(2,1)} %upstream_in.1, bf16[2048,2048]{1,0:T(8,128)(2,1)} %query_weight.1, ...), custom_call_target="tpu_custom_call" | custom-call | tf_op jit(solution)/shard_map/pallas_call | solution.py:1062
  190.9 2.6 %shard_map.164 = (bf16[256,2048]{1,0:T(8,128)(2,1)}, f32[48,2048]{1,0:T(8,128)}, f32[16,2048]{1,0:T(8,128)}, f32[2,16,256]{2,1,0:T(8,128)}, f32[16,2048]{1,0:T(8,128)}, /*index=5*/f32[16,2048]{1,0:T(8,128)}) custom-call(bf16[256,2048]{1,0:T(8,128)(2,1)} %get-tuple-element.18.refs_0_, f32[48,2048]{1,0:T(8,128)} %get-tuple-element.19.refs_1_, ...), custom_call_target="tpu_custom_call" | custom-call | tf_op jit(solution)/shard_map/pallas_call | solution.py:1132
